TPU v7x, 32 devices: a whole 2x2x4 slice. The times are simulated.
32 devices in a mesh: grp: 2 (over y), lat: 4 (over z), lon: 2 (over x), ch: 2 (over core).
Axes of the slice: x: 2, y: 2, z: 4, core: 2. Of those that a mesh axis runs over, the one named last changes fastest.
Arguments:
- noisy_state: bfloat16 [256, 32, 512], P(('grp', 'ch'), 'lat', 'lon'), parts along dimension 0, may hold values from -6 to 6
- kernel_in: bfloat16 [3, 3, 128, 128], replicated, may hold values from -0.1875 to 0.1875
- bias_in: float32 [128], replicated, may hold values from -4 to 4
- kernel_out: bfloat16 [3, 3, 128, 128], replicated, may hold values from -0.1875 to 0.1875
- interp_weight: bfloat16 [64, 128, 128], P(('grp', 'lat', 'lon')), parts along dimension 0, may hold values from -0.5 to 0.5
- observed: bfloat16 [64, 128, 128], P(('grp', 'lat', 'lon'), 'ch'), parts along dimension 0, may hold values from -6 to 6
- obs_precision: bfloat16 [64, 128], P(('grp', 'lat', 'lon')), parts along dimension 0, may hold values from 0.29882812 to 3
- dest_tile: int32 [64], P(('grp', 'lat', 'lon')), parts along dimension 0, may hold values from 0 to 3, as said below
- row_offset: int32 [64], P(('grp', 'lat', 'lon')), parts along dimension 0, may hold values from 0 to 4
- col_offset: int32 [64], P(('grp', 'lat', 'lon')), parts along dimension 0, may hold values from 0 to 224
Outputs:
- next_state: float32 [256, 32, 512], P(('grp', 'ch'), 'lat', 'lon'), parts along dimension 0
- innovation: bfloat16 [64, 128, 128], P(('grp', 'lat', 'lon'), 'ch'), parts along dimension 0
There are 2 independent parts, one for each index of `grp`. A program takes and returns all parts, laid end to end along the dimension named above; an argument that names none is the same for every part. Nothing has to cross between parts.
Inputs may be any that keep to these rules, and one draw needn't show every extreme that they name: `dest_tile`: the 4 blocks of one device name any one latitude tile at most 2 times; a block's tile lies in the longitude column of the device that holds the block.
All inputs are finite; a program needn't handle non-finite values.
Results may differ from a plain program's by a relative error of at most 0.0085.
Values may be sent and summed in bfloat16 or wider, within the bound.
A program may use at most 64 MiB of HBM per device.

v0:
```python
import functools

import jax
import jax.numpy as jnp
from jax import lax
from jax.experimental import pallas as pl
from jax.experimental.pallas import tpu as pltpu
from jax.sharding import PartitionSpec as P

PH = 4
PW = 32
CAP = 2
HALO = 2
SIDE = 16
META = 16
GROUP = 8

keep_rate = 0.6
blend_rate = 0.4
guide_rate = 0.3

MESH = pl.DeviceIdType.MESH
F32 = jnp.float32
BF16 = jnp.bfloat16


def kernel(
    n_lat, n_lon, rows, width, half, blocks,
    dest, row_off, col_off, x_hbm, kin_hbm, kout_hbm, bias, weight_hbm, values_hbm, scale_hbm,
    out, inn_out,
    xv, xs, x_send, kin, kout, weight, values, scale_raw, scale, kfi, kfo, load_sem,
    both, X, X3, H3, pre, base, D, E, pay, R, G, GF, inn, inn_r, out_s, out_r, pulled_s,
    plan,
    halo_s, halo_r, pair_s, pair_r, pay_s, pay_r, inn_ss, inn_rs,
):
    lat, lon, ch = lax.axis_index("lat"), lax.axis_index("lon"), lax.axis_index("ch")
    other = 1 - ch
    chans = 2 * half
    obs = weight_hbm.shape[1]
    cells = PH * PW
    pitch = width + 2 * SIDE
    slots = n_lat * CAP
    px = rows * width
    lon_right = lax.rem(lon + ch, n_lon)
    lon_left = lax.rem(lon + n_lon - other, n_lon)
    has_up = lat > 0
    has_down = lat < n_lat - 1
    sibling = {"ch": other}

    def at(dlat, side):
        place = {"lat": lat + dlat}
        if side:
            place["lon"] = lon_right if side > 0 else lon_left
            place["ch"] = other
        return place

    loads = [
        pltpu.make_async_copy(src, dst, load_sem.at[i])
        for i, (src, dst) in enumerate(
            [(x_hbm, xv), (weight_hbm, weight), (values_hbm, values), (scale_hbm, scale_raw),
             (kin_hbm, kin), (kout_hbm, kout)]
        )
    ]
    for load in loads:
        load.start()
    barrier = pltpu.get_barrier_semaphore()

    def greet(place):
        pl.semaphore_signal(barrier, inc=1, device_id=place, device_id_type=MESH)

    for step in range(1, n_lat):
        greet({"lat": lax.rem(lat + step, n_lat)})
    greet(at(0, -1))
    greet(at(0, 1))

    @pl.when(has_up)
    def _():
        greet(at(-1, -1))
        greet(at(-1, 1))

    @pl.when(has_down)
    def _():
        greet(at(1, -1))
        greet(at(1, 1))

    def count_block(b, _):
        def earlier(e, rank):
            return rank + jnp.where(dest[e] == dest[b], 1, 0)

        plan[b] = dest[b] * CAP + lax.fori_loop(0, b, earlier, 0)
        return 0

    for b in range(blocks) if blocks <= 8 else ():
        rank = 0
        for e in range(b):
            rank = rank + jnp.where(dest[e] == dest[b], 1, 0)
        plan[b] = dest[b] * CAP + rank
    if blocks > 8:
        lax.fori_loop(0, blocks, count_block, 0)

    def pack_slot(s, _):
        def look(b, found):
            return jnp.where(plan[b] == s, b, found)

        found = lax.fori_loop(0, blocks, look, -1)
        source = jnp.maximum(found, 0)
        fill = jnp.where(found >= 0, 1.0, 0.0)
        w = (weight[source].astype(F32) * fill).astype(BF16)
        t = s // CAP
        k = s % CAP
        pay[t, k, 0:half] = w_half(w)
        pay[t, k, half:chans] = values[source]
        level = lax.broadcasted_iota(jnp.int32, (META, obs), 0)
        r0 = row_off[source].astype(F32)
        q0 = col_off[source].astype(F32)
        meta = jnp.where(level == 0, scale[pl.ds(source, 1), :], jnp.where(level == 1, r0, q0))
        pay[t, k, chans : chans + META] = meta.astype(BF16)
        return 0

    def w_half(w):
        return jnp.where(ch == 0, w[0:half].astype(F32), w[half:chans].astype(F32)).astype(BF16)

    loads[0].wait()
    for h in range(2):
        part = xv[:, :, h * width : (h + 1) * width].astype(F32)
        xs[h] = part.reshape(half * rows, width)
    for r in range(rows):
        both[ch, r] = xs[ch, pl.ds(r, half, stride=rows), :].astype(BF16)
        x_send[r] = xs[other, pl.ds(r, half, stride=rows), :].astype(BF16)

    tops = (lat + n_lat - 1) // n_lat
    bottoms = (2 * n_lat - 2 - lat) // n_lat
    pl.semaphore_wait(barrier, n_lat + 1 + 2 * tops + 2 * bottoms)

    def pair_copy(src, dst, i):
        return pltpu.make_async_remote_copy(
            src_ref=src, dst_ref=dst, send_sem=pair_s.at[i], recv_sem=pair_r.at[i],
            device_id=sibling, device_id_type=MESH,
        )

    reshard = pair_copy(x_send, both.at[ch], 0)
    reshard.start()
    for load in loads[1:4]:
        load.wait()
    scale[...] = scale_raw[...].astype(F32)
    lax.fori_loop(0, slots, pack_slot, 0)

    top, left = HALO, SIDE
    spans_r = {-1: (top, 0 + rows + top), 0: (top, top), 1: (top + rows - HALO, 0)}
    spans_c = {-1: (left, left + width), 0: (left, left), 1: (left + width - SIDE, 0)}
    size_r = {-1: HALO, 0: rows, 1: HALO}
    size_c = {-1: SIDE, 0: width, 1: SIDE}
    routes = [(0, -1), (0, 1), (-1, 0), (-1, -1), (-1, 1), (1, 0), (1, -1), (1, 1)]

    def halo_copy(buf, i, base_sem):
        dl, side = routes[i]
        sr, dr = spans_r[dl]
        sc, dc = spans_c[side]
        src = buf.at[pl.ds(sr, size_r[dl]), pl.ds(sc, size_c[side])]
        dst = buf.at[pl.ds(dr, size_r[dl]), pl.ds(dc, size_c[side])]
        return pltpu.make_async_remote_copy(
            src_ref=src, dst_ref=dst,
            send_sem=halo_s.at[base_sem + i], recv_sem=halo_r.at[base_sem + i],
            device_id=at(dl, side), device_id_type=MESH,
        )

    def halo_wait_recv(buf, i, base_sem):
        halo_copy(buf, i, base_sem).wait_recv()

    def guarded(dl, fn):
        if dl == 0:
            fn()
        else:
            pl.when(has_up if dl < 0 else has_down)(fn)

    def halo_start(buf, base_sem):
        for dl in (-1, 1, 0):
            def go(dl=dl):
                for i, route in enumerate(routes):
                    if route[0] == dl:
                        halo_copy(buf, i, base_sem).start()

            guarded(dl, go)

    def halo_finish(buf, base_sem, rows_of):
        for dl in rows_of:
            def go(dl=dl):
                for i, route in enumerate(routes):
                    if route[0] == dl:
                        halo_copy(buf, i, base_sem).wait_send()

            def got(dl=dl):
                for i, route in enumerate(routes):
                    if route[0] == dl:
                        halo_wait_recv(buf, i, base_sem)

            guarded(dl, go)
            guarded(-dl, got)

    def rim_conv(buf, base_sem, step):
        halo_finish(buf, base_sem, (0,))
        for r in range(HALO, HALO + rows):
            put_row(X3, r, buf[r].astype(F32))
        for r0 in range(HALO, rows, CH):
            step(r0)
        halo_finish(buf, base_sem, (-1, 1))
        for r in (0, 1, HALO + rows, HALO + rows + 1):
            put_row(X3, r, buf[r].astype(F32))
        for r0 in (0, rows):
            step(r0)

    CH = 2
    WIDE = 4

    def clear_poles(buf):
        @pl.when(lat == 0)
        def _():
            buf[0:HALO] = jnp.zeros((HALO, pitch, chans), BF16)

        @pl.when(lat == n_lat - 1)
        def _():
            buf[rows + HALO : rows + 2 * HALO] = jnp.zeros((HALO, pitch, chans), BF16)

    def put_row(taps, r, v):
        taps[r * pitch : (r + 1) * pitch, 0:chans] = pltpu.roll(v, 1, 0).astype(BF16)
        taps[r * pitch : (r + 1) * pitch, chans : 2 * chans] = v.astype(BF16)
        taps[r * pitch : (r + 1) * pitch, 2 * chans :] = pltpu.roll(v, pitch - 1, 0).astype(BF16)

    def conv(taps, kmat, first, count):
        acc = None
        for a in range(3):
            part = jnp.dot(
                taps[(first + a) * pitch : (first + a + count) * pitch, :], kmat(a),
                preferred_element_type=F32,
            )
            acc = part if acc is None else acc + part
        return acc

    def mirrored(k, a):
        return jnp.concatenate([k[2 - a, 2], k[2 - a, 1], k[2 - a, 0]], axis=0)

    def edge_factor(r):
        if r == 0:
            return jnp.where(has_up, 1.0, 0.0)
        if r == rows + 1:
            return jnp.where(has_down, 1.0, 0.0)
        return None

    clear_poles(X)
    clear_poles(G)

    reshard.wait()
    for r in range(rows):
        X[top + r, left : left + width] = (
            jnp.concatenate([both[0, r], both[1, r]], axis=0).astype(F32).T.astype(BF16)
        )
    halo_start(X, 0)

    def pay_copy(i, step):
        peer = lax.rem(lat + step, n_lat)
        return pltpu.make_async_remote_copy(
            src_ref=pay.at[peer], dst_ref=R.at[lat, ch],
            send_sem=pay_s.at[i], recv_sem=pay_r.at[i],
            device_id={"lat": peer}, device_id_type=MESH,
        )

    for step in range(1, n_lat):
        pay_copy(step - 1, step).start()
    R[lat, ch] = pay[lat]
    for load in loads[4:]:
        load.wait()
    for a in range(3):
        for b in range(3):
            kfi[a, b * chans : (b + 1) * chans] = kin[a, b].astype(F32).T.astype(BF16)
            kfo[a, b * chans : (b + 1) * chans] = kout[a, b].astype(F32).T.astype(BF16)

    def hidden_rows(r0):
        acc = conv(X3, lambda a: kfi[a], r0, CH) + bias[...]
        pre[r0 * pitch : (r0 + CH) * pitch, :] = acc
        h = acc / (1.0 + jnp.exp(-acc))
        for i in range(CH):
            row = h[i * pitch : (i + 1) * pitch]
            f = edge_factor(r0 + i)
            if f is not None:
                row = row * f
            put_row(H3, r0 + i, row.astype(BF16).astype(F32))

    rim_conv(X, 0, hidden_rows)

    for r0 in range(0, rows, WIDE):
        acc = conv(H3, lambda a: kfo[a], r0, WIDE)
        for i in range(WIDE):
            r = r0 + i
            state = X[top + r, left : left + width].astype(F32)
            den = (state + acc[i * pitch + left : i * pitch + left + width]).astype(BF16)
            base[r * width : (r + 1) * width, :] = keep_rate * state + blend_rate * den.astype(F32)
            D[ch, :, r * width : (r + 1) * width] = den.astype(F32).T.astype(BF16)
    swap = pair_copy(D.at[ch], D.at[ch], 2)
    swap.start()

    for step in range(1, n_lat):
        pay_copy(step - 1, step).wait()
    forward = pair_copy(R.at[:, ch], R.at[:, ch], 1)
    forward.start()

    lane = lax.broadcasted_iota(jnp.int32, (1, cells), 1)
    cell_r = (lane // PW).astype(F32)
    cell_c = (lane % PW).astype(F32)

    def each_group(fn):
        if slots == GROUP:
            fn(0)
        else:
            lax.fori_loop(0, slots // GROUP, lambda g, _: fn(g) or 0, 0)

    def place_group(g):
        def place_rows(n, _):
            index = lax.broadcasted_iota(jnp.int32, (width, cells), 0) + n * width
            index = index.astype(F32)
            for i in range(GROUP):
                s = g * GROUP + i
                meta = R[s // CAP, ch, s % CAP, chans : chans + META].astype(F32)
                q = meta[2:3] + cell_c
                target = (meta[1:2] + cell_r) * width + q
                target = target + jnp.where(q >= width, float(px - width), 0.0)
                E[g, pl.ds(pl.multiple_of(n * width, width), width), i * cells : (i + 1) * cells] = (
                    jnp.where(index == target, 1.0, 0.0).astype(BF16)
                )
            return 0

        lax.fori_loop(0, 2 * rows, place_rows, 0)

    each_group(place_group)
    forward.wait()
    swap.wait()

    def observe_group(g):
        patches = jnp.dot(D[0], E[g, 0:px], preferred_element_type=F32) + jnp.dot(
            D[1], E[g, px : 2 * px], preferred_element_type=F32
        )
        patches = patches.astype(BF16)
        for i in range(GROUP):
            s = g * GROUP + i
            t = s // CAP
            k = s % CAP
            own = slice(i * cells, (i + 1) * cells)
            w = jnp.concatenate([R[t, 0, k, 0:half], R[t, 1, k, 0:half]], axis=0)
            val = jnp.concatenate([R[t, 0, k, half:chans], R[t, 1, k, half:chans]], axis=0)
            predicted = lax.dot_general(
                patches[:, own], w, (((1,), (1,)), ((), ())), preferred_element_type=F32
            )
            residual = predicted - val.astype(F32)
            inn[t, k] = jnp.where(ch == 0, residual[0:half], residual[half:chans]).astype(BF16)
            sc = R[t, 0, k, chans : chans + META].astype(F32)[0:1]
            weighted = (residual * sc).astype(BF16)
            pulled_s[g, :, own] = jnp.dot(weighted, w, preferred_element_type=F32).astype(BF16)

    each_group(observe_group)

    def spread_group(g):
        added = lax.dot_general(
            E[g, pl.ds(pl.multiple_of(ch * px, px), px)], pulled_s[g],
            (((1,), (1,)), ((), ())), preferred_element_type=F32,
        )
        if slots == GROUP:
            GF[...] = added
        else:
            GF[...] += added

    if slots != GROUP:
        GF[...] = jnp.zeros((px, chans), F32)
    each_group(spread_group)
    for r in range(rows):
        G[top + r, left : left + width] = GF[r * width : (r + 1) * width, :].astype(BF16)
    halo_start(G, 8)

    def inn_copy(i, step):
        peer = lax.rem(lat + step, n_lat)
        return pltpu.make_async_remote_copy(
            src_ref=inn.at[peer], dst_ref=inn_r.at[lat],
            send_sem=inn_ss.at[i], recv_sem=inn_rs.at[i],
            device_id={"lat": peer}, device_id_type=MESH,
        )

    for step in range(1, n_lat):
        inn_copy(step - 1, step).start()
    inn_r[lat] = inn[lat]

    def grad_rows(r0):
        back = conv(X3, lambda a: mirrored(kout, a), r0, CH)
        v = pre[r0 * pitch : (r0 + CH) * pitch, :]
        s = 1.0 / (1.0 + jnp.exp(-v))
        g = back * s * (1.0 + v * (1.0 - s))
        for i in range(CH):
            row = g[i * pitch : (i + 1) * pitch]
            f = edge_factor(r0 + i)
            if f is not None:
                row = row * f
            put_row(H3, r0 + i, row.astype(BF16).astype(F32))

    rim_conv(G, 8, grad_rows)
    for r0 in range(0, rows, WIDE):
        acc = conv(H3, lambda a: mirrored(kin, a), r0, WIDE)
        for i in range(WIDE):
            r = r0 + i
            own = slice(r * width, (r + 1) * width)
            grad = GF[own, :] + acc[i * pitch + left : i * pitch + left + width]
            res = (base[own, :] - guide_rate * grad).T
            out_s[0, pl.ds(r, half, stride=rows), :] = res[0:half]
            out_s[1, pl.ds(r, half, stride=rows), :] = res[half:chans]
    back_home = pair_copy(out_s.at[other], out_r, 3)
    back_home.start()
    out[ch] = out_s[ch]
    for step in range(1, n_lat):
        inn_copy(step - 1, step).wait()

    def fetch(b, _):
        slot = plan[b]
        inn_out[b] = inn_r[slot // CAP, slot % CAP]
        return 0

    lax.fori_loop(0, blocks, fetch, 0)
    back_home.wait()
    out[other] = out_r[...]


def body(n_lat, n_lon, noisy_state, kernel_in, bias_in, kernel_out, interp_weight, observed,
         obs_precision, dest_tile, row_offset, col_offset):
    half, rows, cols = noisy_state.shape
    chans = 2 * half
    width = cols // 2
    blocks, obs, cells = interp_weight.shape
    slots = n_lat * CAP
    pitch = width + 2 * SIDE
    px = rows * width
    vmem = pl.BlockSpec(memory_space=pltpu.VMEM)
    hbm = pl.BlockSpec(memory_space=pltpu.HBM)
    smem = pl.BlockSpec(memory_space=pltpu.SMEM)
    call = pl.pallas_call(
        functools.partial(kernel, n_lat, n_lon, rows, width, half, blocks),
        out_shape=(
            jax.ShapeDtypeStruct((2, half * rows, width), F32),
            jax.ShapeDtypeStruct((blocks, half, obs), BF16),
        ),
        in_specs=[smem] * 3 + [hbm] * 3 + [vmem] + [hbm] * 3,
        out_specs=(vmem, vmem),
        scratch_shapes=[
            pltpu.VMEM((half, rows, cols), BF16),
            pltpu.VMEM((2, half * rows, width), F32),
            pltpu.VMEM((rows, half, width), BF16),
            pltpu.VMEM(kernel_in.shape, BF16),
            pltpu.VMEM(kernel_out.shape, BF16),
            pltpu.VMEM(interp_weight.shape, BF16),
            pltpu.VMEM(observed.shape, BF16),
            pltpu.VMEM(obs_precision.shape, BF16),
            pltpu.VMEM(obs_precision.shape, F32),
            pltpu.VMEM((3, 3 * chans, chans), BF16),
            pltpu.VMEM((3, 3 * chans, chans), BF16),
            pltpu.SemaphoreType.DMA((6,)),
            pltpu.VMEM((2, rows, half, width), BF16),
            pltpu.VMEM((rows + 4, pitch, chans), BF16),
            pltpu.VMEM(((rows + 4) * pitch, 3 * chans), BF16),
            pltpu.VMEM(((rows + 2) * pitch, 3 * chans), BF16),
            pltpu.VMEM(((rows + 2) * pitch, chans), F32),
            pltpu.VMEM((px, chans), F32),
            pltpu.VMEM((2, chans, px), BF16),
            pltpu.VMEM((slots // GROUP, 2 * px, GROUP * cells), BF16),
            pltpu.VMEM((n_lat, CAP, chans + META, obs), BF16),
            pltpu.VMEM((n_lat, 2, CAP, chans + META, obs), BF16),
            pltpu.VMEM((rows + 4, pitch, chans), BF16),
            pltpu.VMEM((px, chans), F32),
            pltpu.VMEM((n_lat, CAP, half, obs), BF16),
            pltpu.VMEM((n_lat, CAP, half, obs), BF16),
            pltpu.VMEM((2, half * rows, width), F32),
            pltpu.VMEM((half * rows, width), F32),
            pltpu.VMEM((slots // GROUP, chans, GROUP * cells), BF16),
            pltpu.SMEM((blocks,), jnp.int32),
            pltpu.SemaphoreType.DMA((16,)),
            pltpu.SemaphoreType.DMA((16,)),
            pltpu.SemaphoreType.DMA((4,)),
            pltpu.SemaphoreType.DMA((4,)),
            pltpu.SemaphoreType.DMA((n_lat - 1,)),
            pltpu.SemaphoreType.DMA((n_lat - 1,)),
            pltpu.SemaphoreType.DMA((n_lat - 1,)),
            pltpu.SemaphoreType.DMA((n_lat - 1,)),
        ],
        compiler_params=pltpu.CompilerParams(
            collective_id=0, has_side_effects=True, vmem_limit_bytes=63 * 1024 * 1024
        ),
    )
    out, innovation = call(
        dest_tile, row_offset, col_offset, noisy_state, kernel_in, kernel_out,
        bias_in.reshape(1, chans), interp_weight, observed, obs_precision,
    )
    next_state = jnp.transpose(out.reshape(2, half, rows, width), (1, 2, 0, 3))
    return next_state.reshape(half, rows, cols), innovation


def solution(mesh):
    return jax.shard_map(
        functools.partial(body, mesh.shape["lat"], mesh.shape["lon"]),
        mesh=mesh,
        in_specs=(
            P(("grp", "ch"), "lat", "lon"),
            P(),
            P(),
            P(),
            P(("grp", "lat", "lon"), None, None),
            P(("grp", "lat", "lon"), "ch", None),
            P(("grp", "lat", "lon"), None),
            P(("grp", "lat", "lon")),
            P(("grp", "lat", "lon")),
            P(("grp", "lat", "lon")),
        ),
        out_specs=(P(("grp", "ch"), "lat", "lon"), P(("grp", "lat", "lon"), "ch", None)),
        check_vma=False,
    )
```

profile of v0, /device:TPU:0, one launch (start us, length us, event | category | flops | bytes accessed | tf_op | source)
XLA Modules:
  0.0 33.5 jit_solution(5917264663757596884)
XLA Ops:
  0.6 30.4 %shard_map.113 = (f32[2,512,128]{2,1,0:T(8,128)}, bf16[4,64,128]{2,1,0:T(8,128)(2,1)}) custom-call(s32[4]{0:T(128)} %dest.1, s32[4]{0:T(128)} %row_off.1, s32[4]{0:T(128)} %col_off.1, bf16[64,8,256]{2,1,0:T(8,128)(2,1)} %x_hbm.1, bf16[3,3,128,128]{3,2,1,0:T(8,128)(2,1)} %kin_hbm.1, bf16[3,3,128,128]{3,2,1,0:T(8,128)(2,1)} %kout_hbm.1, f32[1,128]{1,0:T(1,128)} %bitcast.8, ...), custom_call_target="tpu_custom_call" | custom-call | tf_op jit(solution)/shard_map/pallas_call | solution.py:491
  31.0 0.0 copy-start
  31.0 1.9 %copy_bitcast_fusion = f32[64,8,256]{2,1,0:T(8,128)} fusion(f32[2,512,128]{2,1,0:T(8,128)} %get-tuple-element.4), kind=kLoop, calls=%fused_computation | loop fusion | bytes 1048576 | tf_op jit(solution)/shard_map/reshape | solution.py:496
  32.9 0.0 copy-done
  32.9 0.6 %copy.15 = bf16[4,64,128]{2,1,0:T(8,128)(2,1)} copy(bf16[4,64,128]{2,1,0:T(8,128)(2,1)S(1)} %copy-done) | data formatting | bytes 131072
Async XLA Ops:
  31.0 1.9 %copy-start = (bf16[4,64,128]{2,1,0:T(8,128)(2,1)S(1)}, bf16[4,64,128]{2,1,0:T(8,128)(2,1)}, u32[]{:S(2)}) copy-start(bf16[4,64,128]{2,1,0:T(8,128)(2,1)} %get-tuple-element.9) | copy-start | bytes 196612
where the time goes:
time: 33.7 us; the launch traced here: 33.5 us
  Pallas kernels  30.4 us (90%)
  local copies, waits for them, and re-layouts  2.54 us (8%)
  between operations  0.65 us (2%)
    pallas_call x1, Pallas kernels, body(): call(dest_tile, row_offset, col_offset, noisy_state, kernel_in, kernel_ou...  30.4 us
    reshape x1, local copies, waits for them, and re-layouts, body(): return (next_state.reshape(half, rows, cols), innovation)  1.9 us

commit v1 on v0

--- a/solution.py
+++ b/solution.py
@@ -14,6 +14,7 @@
 SIDE = 16
 META = 16
 GROUP = 8
+WIDE = 4
 
 keep_rate = 0.6
 blend_rate = 0.4
@@ -29,8 +30,8 @@
     dest, row_off, col_off, x_hbm, kin_hbm, kout_hbm, bias, weight_hbm, values_hbm, scale_hbm,
     out, inn_out,
     xv, xs, x_send, kin, kout, weight, values, scale_raw, scale, kfi, kfo, load_sem,
-    both, X, X3, H3, pre, base, D, E, pay, R, G, GF, inn, inn_r, out_s, out_r, pulled_s,
-    plan,
+    both, X, X3, H3, pre, base, D, E, pay, R, G, GF, inn, inn_r, out_h, out_s, out_r, pulled_s,
+    plan, heard_up, heard_down,
     halo_s, halo_r, pair_s, pair_r, pay_s, pay_r, inn_ss, inn_rs,
 ):
     lat, lon, ch = lax.axis_index("lat"), lax.axis_index("lon"), lax.axis_index("ch")
@@ -68,20 +69,18 @@
     def greet(place):
         pl.semaphore_signal(barrier, inc=1, device_id=place, device_id_type=MESH)
 
-    for step in range(1, n_lat):
-        greet({"lat": lax.rem(lat + step, n_lat)})
     greet(at(0, -1))
     greet(at(0, 1))
 
     @pl.when(has_up)
     def _():
-        greet(at(-1, -1))
-        greet(at(-1, 1))
+        for side in (-1, 0, 1):
+            greet(at(-1, side))
 
     @pl.when(has_down)
     def _():
-        greet(at(1, -1))
-        greet(at(1, 1))
+        for side in (-1, 0, 1):
+            greet(at(1, side))
 
     def count_block(b, _):
         def earlier(e, rank):
@@ -130,7 +129,18 @@
 
     tops = (lat + n_lat - 1) // n_lat
     bottoms = (2 * n_lat - 2 - lat) // n_lat
-    pl.semaphore_wait(barrier, n_lat + 1 + 2 * tops + 2 * bottoms)
+    pl.semaphore_wait(barrier, 2 + 3 * tops + 3 * bottoms)
+
+    def tell(sem, dlat):
+        pl.semaphore_signal(sem, inc=1, device_id={"lat": lat + dlat}, device_id_type=MESH)
+
+    @pl.when((lat == 1) & has_down)
+    def _():
+        tell(heard_up, 1)
+
+    @pl.when((lat == n_lat - 2) & has_up)
+    def _():
+        tell(heard_down, -1)
 
     def pair_copy(src, dst, i):
         return pltpu.make_async_remote_copy(
@@ -210,7 +220,6 @@
             step(r0)
 
     CH = 2
-    WIDE = 4
 
     def clear_poles(buf):
         @pl.when(lat == 0)
@@ -264,8 +273,35 @@
             device_id={"lat": peer}, device_id_type=MESH,
         )
 
+    def is_near(step):
+        peer = lax.rem(lat + step, n_lat)
+        return (peer == lat + 1) | (peer == lat - 1)
+
     for step in range(1, n_lat):
-        pay_copy(step - 1, step).start()
+        @pl.when(is_near(step))
+        def _(step=step):
+            pay_copy(step - 1, step).start()
+
+    @pl.when(lat >= 2)
+    def _():
+        pl.semaphore_wait(heard_up, 1)
+
+        @pl.when(has_down)
+        def _():
+            tell(heard_up, 1)
+
+    @pl.when(lat <= n_lat - 3)
+    def _():
+        pl.semaphore_wait(heard_down, 1)
+
+        @pl.when(has_up)
+        def _():
+            tell(heard_down, -1)
+
+    for step in range(1, n_lat):
+        @pl.when(jnp.logical_not(is_near(step)))
+        def _(step=step):
+            pay_copy(step - 1, step).start()
     R[lat, ch] = pay[lat]
     for load in loads[4:]:
         load.wait()
@@ -399,6 +435,9 @@
             put_row(H3, r0 + i, row.astype(BF16).astype(F32))
 
     rim_conv(G, 8, grad_rows)
+    mine = pl.ds(pl.multiple_of(ch * width, width), width)
+    theirs = pl.ds(pl.multiple_of(other * width, width), width)
+    back_home = []
     for r0 in range(0, rows, WIDE):
         acc = conv(H3, lambda a: mirrored(kin, a), r0, WIDE)
         for i in range(WIDE):
@@ -406,11 +445,12 @@
             own = slice(r * width, (r + 1) * width)
             grad = GF[own, :] + acc[i * pitch + left : i * pitch + left + width]
             res = (base[own, :] - guide_rate * grad).T
-            out_s[0, pl.ds(r, half, stride=rows), :] = res[0:half]
-            out_s[1, pl.ds(r, half, stride=rows), :] = res[half:chans]
-    back_home = pair_copy(out_s.at[other], out_r, 3)
-    back_home.start()
-    out[ch] = out_s[ch]
+            out_h[0, pl.ds(r, half, stride=rows), :] = jnp.where(ch == 0, res[0:half], res[half:chans])
+            out_s[r] = jnp.where(ch == 0, res[half:chans], res[0:half]).astype(BF16)
+        sent = pl.ds(r0, WIDE)
+        back_home.append(pair_copy(out_s.at[sent], out_r.at[sent], 3 + r0 // WIDE))
+        back_home[-1].start()
+    out[:, mine] = out_h[0]
     for step in range(1, n_lat):
         inn_copy(step - 1, step).wait()
 
@@ -420,8 +460,11 @@
         return 0
 
     lax.fori_loop(0, blocks, fetch, 0)
-    back_home.wait()
-    out[other] = out_r[...]
+    for i, copy in enumerate(back_home):
+        copy.wait()
+        for r in range(i * WIDE, (i + 1) * WIDE):
+            out_h[1, pl.ds(r, half, stride=rows), :] = out_r[r].astype(F32)
+    out[:, theirs] = out_h[1]
 
 
 def body(n_lat, n_lon, noisy_state, kernel_in, bias_in, kernel_out, interp_weight, observed,
@@ -436,11 +479,12 @@
     vmem = pl.BlockSpec(memory_space=pltpu.VMEM)
     hbm = pl.BlockSpec(memory_space=pltpu.HBM)
     smem = pl.BlockSpec(memory_space=pltpu.SMEM)
+    place = pltpu.VMEM if slots <= GROUP else jax.ShapeDtypeStruct
     call = pl.pallas_call(
         functools.partial(kernel, n_lat, n_lon, rows, width, half, blocks),
         out_shape=(
-            jax.ShapeDtypeStruct((2, half * rows, width), F32),
-            jax.ShapeDtypeStruct((blocks, half, obs), BF16),
+            place((half * rows, cols), F32),
+            place((blocks, half, obs), BF16),
         ),
         in_specs=[smem] * 3 + [hbm] * 3 + [vmem] + [hbm] * 3,
         out_specs=(vmem, vmem),
@@ -472,13 +516,16 @@
             pltpu.VMEM((n_lat, CAP, half, obs), BF16),
             pltpu.VMEM((n_lat, CAP, half, obs), BF16),
             pltpu.VMEM((2, half * rows, width), F32),
-            pltpu.VMEM((half * rows, width), F32),
+            pltpu.VMEM((rows, half, width), BF16),
+            pltpu.VMEM((rows, half, width), BF16),
             pltpu.VMEM((slots // GROUP, chans, GROUP * cells), BF16),
             pltpu.SMEM((blocks,), jnp.int32),
+            pltpu.SemaphoreType.REGULAR,
+            pltpu.SemaphoreType.REGULAR,
             pltpu.SemaphoreType.DMA((16,)),
             pltpu.SemaphoreType.DMA((16,)),
-            pltpu.SemaphoreType.DMA((4,)),
-            pltpu.SemaphoreType.DMA((4,)),
+            pltpu.SemaphoreType.DMA((3 + rows // WIDE,)),
+            pltpu.SemaphoreType.DMA((3 + rows // WIDE,)),
             pltpu.SemaphoreType.DMA((n_lat - 1,)),
             pltpu.SemaphoreType.DMA((n_lat - 1,)),
             pltpu.SemaphoreType.DMA((n_lat - 1,)),
@@ -492,8 +539,7 @@
         dest_tile, row_offset, col_offset, noisy_state, kernel_in, kernel_out,
         bias_in.reshape(1, chans), interp_weight, observed, obs_precision,
     )
-    next_state = jnp.transpose(out.reshape(2, half, rows, width), (1, 2, 0, 3))
-    return next_state.reshape(half, rows, cols), innovation
+    return out.reshape(half, rows, cols), innovation
 
 
 def solution(mesh):

time: 33.7 us -> 31.1 us (0.923)
  Pallas kernels: 30.4 us -> 28.9 us
  local copies, waits for them, and re-layouts: 2.54 us -> 1.42 us
    reshape x1 -> x0, local copies, waits for them, and re-layouts: 1.9 us -> none  [body(): return (next_state.reshape(half, rows, cols), innovation)]
    pallas_call x1, Pallas kernels: 30.4 us -> 28.9 us  [body(): call(dest_tile, row_offset, col_offset, noisy_state, kernel_in, kernel_ou...]
    unnamed x3 -> x2, local copies, waits for them, and re-layouts: 0.63 us -> 1.42 us
where the time goes in v1:
time: 31.1 us; the launch traced here: 30.9 us
  Pallas kernels  28.9 us (93%)
  local copies, waits for them, and re-layouts  1.42 us (5%)
  between operations  0.64 us (2%)
    pallas_call x1, Pallas kernels, body(): call(dest_tile, row_offset, col_offset, noisy_state, kernel_in, kernel_ou...  28.9 us
    unnamed x2, local copies, waits for them, and re-layouts  1.42 us

profile of v1, /device:TPU:0, one launch (start us, length us, event | category | flops | bytes accessed | tf_op | source)
XLA Modules:
  0.0 30.9 jit_solution(5946852777787834129)
XLA Ops:
  0.6 28.9 %shard_map.113 = (f32[512,256]{1,0:T(8,128)S(1)}, bf16[4,64,128]{2,1,0:T(8,128)(2,1)S(1)}) custom-call(s32[4]{0:T(128)} %dest.1, s32[4]{0:T(128)} %row_off.1, s32[4]{0:T(128)} %col_off.1, bf16[64,8,256]{2,1,0:T(8,128)(2,1)} %x_hbm.1, bf16[3,3,128,128]{3,2,1,0:T(8,128)(2,1)} %kin_hbm.1, bf16[3,3,128,128]{3,2,1,0:T(8,128)(2,1)} %kout_hbm.1, f32[1,128]{1,0:T(1,128)} %bitcast.3, ...), custom_call_target="tpu_custom_call" | custom-call | tf_op jit(solution)/shard_map/pallas_call | solution.py:538
  29.5 0.8 %copy.14 = f32[64,8,256]{2,1,0:T(8,128)} copy(f32[64,8,256]{2,1,0:T(8,128)S(1)} %bitcast.2) | data formatting | bytes 1048576
  30.3 0.6 %copy.15 = bf16[4,64,128]{2,1,0:T(8,128)(2,1)} copy(bf16[4,64,128]{2,1,0:T(8,128)(2,1)S(1)} %get-tuple-element.7) | data formatting | bytes 131072

commit v2 on v1

v2 whole, which is shorter than its diff:
```python
import functools

import jax
import jax.numpy as jnp
from jax import lax
from jax.experimental import pallas as pl
from jax.experimental.pallas import tpu as pltpu
from jax.sharding import PartitionSpec as P

PH = 4
PW = 32
CAP = 2
HALO = 2
SIDE = 16
GROUP = 8
WIDE = 4
SMALL = 8

keep_rate = 0.6
blend_rate = 0.4
guide_rate = 0.3

MESH = pl.DeviceIdType.MESH
F32 = jnp.float32
BF16 = jnp.bfloat16
I32 = jnp.int32


def sigmoid(v):
    return 0.5 + 0.5 * jnp.tanh(0.5 * v)


def each(count, fn):
    if count <= 8:
        for i in range(count):
            fn(i)
    else:
        lax.fori_loop(0, count, lambda i, _: fn(i) or 0, 0)


def kernel(
    n_lat, n_lon, rows, width, half, blocks,
    dest, row_off, col_off, x_hbm, kin_hbm, kout_hbm, bias, weight_hbm, values_hbm, scale_hbm,
    out, inn_out,
    xv, xs, x_send, kin, kout, weight, values, scale_raw, scale, kw, load_sem,
    both, X, X3, H3, slope, base, DF, den_s, den_r, pay, pay_at, pay_p, R, R_at, R_p, at_s,
    res_t, Z, G, GW, inn, inn_r, out_h, out_s, out_r,
    plan, heard_up, heard_down,
    halo_s, halo_r, pair_s, pair_r, pay_ss, pay_rs, at_ss, at_rs, p_ss, p_rs, fwd_s, fwd_r, copy_sem, inn_ss, inn_rs,
):
    lat, lon, ch = lax.axis_index("lat"), lax.axis_index("lon"), lax.axis_index("ch")
    other = 1 - ch
    chans = 2 * half
    obs = weight_hbm.shape[1]
    cells = PH * PW
    cols = 2 * width
    pitch = width + 2 * SIDE
    reach = width + SIDE
    strip = 2 * reach + PW
    blank = GROUP * PH * strip
    slots = n_lat * CAP
    sources = GROUP // CAP
    px = rows * width
    top, left = HALO, SIDE
    lon_right = lax.rem(lon + ch, n_lon)
    lon_left = lax.rem(lon + n_lon - other, n_lon)
    has_up = lat > 0
    has_down = lat < n_lat - 1
    sibling = {"ch": other}

    def at(dlat, side):
        place = {"lat": lat + dlat}
        if side:
            place["lon"] = lon_right if side > 0 else lon_left
            place["ch"] = other
        return place

    def outward(dlat):
        return {"lat": lat + dlat, "lon": jnp.where(ch == 0, lon_left, lon_right), "ch": other}

    def peer_of(j):
        m = jnp.minimum(lat, n_lat - 1 - lat)
        step = jnp.where(j < 2 * m, j // 2 + 1, j - m + 1)
        below = jnp.where(j < 2 * m, j % 2 == 0, lat > n_lat - 1 - lat)
        return jnp.where(below, lat - step, lat + step)

    loads = [
        pltpu.make_async_copy(src, dst, load_sem.at[i])
        for i, (src, dst) in enumerate(
            [(x_hbm, xv), (weight_hbm, weight), (values_hbm, values), (scale_hbm, scale_raw),
             (kin_hbm, kin), (kout_hbm, kout)]
        )
    ]
    for load in loads:
        load.start()
    barrier = pltpu.get_barrier_semaphore()

    def greet(place):
        pl.semaphore_signal(barrier, inc=1, device_id=place, device_id_type=MESH)

    greet(at(0, -1))
    greet(at(0, 1))

    @pl.when(has_up)
    def _():
        for side in (-1, 0, 1):
            greet(at(-1, side))

    @pl.when(has_down)
    def _():
        for side in (-1, 0, 1):
            greet(at(1, side))

    def count_block(b, _):
        def earlier(e, rank):
            return rank + jnp.where(dest[e] == dest[b], 1, 0)

        plan[b] = dest[b] * CAP + lax.fori_loop(0, b, earlier, 0)
        return 0

    for b in range(blocks) if blocks <= 8 else ():
        rank = 0
        for e in range(b):
            rank = rank + jnp.where(dest[e] == dest[b], 1, 0)
        plan[b] = dest[b] * CAP + rank
    if blocks > 8:
        lax.fori_loop(0, blocks, count_block, 0)

    def w_half(w):
        return jnp.where(ch == 0, w[0:half].astype(F32), w[half:chans].astype(F32)).astype(BF16)

    def pack_slot(s, _):
        def look(b, found):
            return jnp.where(plan[b] == s, b, found)

        found = lax.fori_loop(0, blocks, look, -1)
        source = jnp.maximum(found, 0)
        fill = jnp.where(found >= 0, 1.0, 0.0)
        w = (weight[source].astype(F32) * fill).astype(BF16)
        t = s // CAP
        k = s % CAP
        pay[t, k, 0:half] = w_half(w)
        pay[t, k, half:chans] = values[source]
        pay_p[t, pl.ds(k, 1), :] = scale[pl.ds(source, 1), :]
        pay_at[t, pl.ds(2 * k, 1), :] = jnp.full((1, obs), row_off[source], I32)
        pay_at[t, pl.ds(2 * k + 1, 1), :] = jnp.full((1, obs), col_off[source], I32)
        return 0

    loads[0].wait()
    for h in range(2):
        part = xv[:, :, h * width : (h + 1) * width].astype(F32)
        xs[h] = part.reshape(half * rows, width)
    for r in range(rows):
        both[ch, r] = xs[ch, pl.ds(r, half, stride=rows), :].astype(BF16)
        x_send[r] = xs[other, pl.ds(r, half, stride=rows), :].astype(BF16)

    tops = (lat + n_lat - 1) // n_lat
    bottoms = (2 * n_lat - 2 - lat) // n_lat
    pl.semaphore_wait(barrier, 2 + 3 * tops + 3 * bottoms)

    def tell(sem, dlat):
        pl.semaphore_signal(sem, inc=1, device_id={"lat": lat + dlat}, device_id_type=MESH)

    @pl.when((lat == 1) & has_down)
    def _():
        tell(heard_up, 1)

    @pl.when((lat == n_lat - 2) & has_up)
    def _():
        tell(heard_down, -1)

    def pair_copy(src, dst, i):
        return pltpu.make_async_remote_copy(
            src_ref=src, dst_ref=dst, send_sem=pair_s.at[i], recv_sem=pair_r.at[i],
            device_id=sibling, device_id_type=MESH,
        )

    reshard = pair_copy(x_send, both.at[ch], 0)
    reshard.start()
    for load in loads[1:4]:
        load.wait()
    scale[...] = scale_raw[...].astype(F32)
    pay_at[...] = jnp.zeros(pay_at.shape, I32)
    pay_p[...] = jnp.zeros(pay_p.shape, F32)
    lax.fori_loop(0, slots, pack_slot, 0)

    def put_row(taps, r, v):
        taps[r * pitch : (r + 1) * pitch, 0:chans] = pltpu.roll(v, 1, 0).astype(BF16)
        taps[r * pitch : (r + 1) * pitch, chans : 2 * chans] = v.astype(BF16)
        taps[r * pitch : (r + 1) * pitch, 2 * chans :] = pltpu.roll(v, pitch - 1, 0).astype(BF16)

    def conv(taps, kind, first, count):
        acc = None
        for a in range(3):
            part = jnp.dot(
                taps[(first + a) * pitch : (first + a + count) * pitch, :], kw[kind, a],
                preferred_element_type=F32,
            )
            acc = part if acc is None else acc + part
        return acc

    def edge_factor(r):
        if r == 0:
            return jnp.where(has_up, 1.0, 0.0)
        if r == rows + 1:
            return jnp.where(has_down, 1.0, 0.0)
        return None

    def guarded(dl, fn):
        if dl == 0:
            fn()
        else:
            pl.when(has_up if dl < 0 else has_down)(fn)

    def span(start, size):
        return pl.ds(start if isinstance(start, int) else pl.multiple_of(start, SIDE), size)

    def remote(buf, place, sr, dr, nr, sc, dc, nc, i):
        return pltpu.make_async_remote_copy(
            src_ref=buf.at[pl.ds(sr, nr), span(sc, nc)], dst_ref=buf.at[pl.ds(dr, nr), span(dc, nc)],
            send_sem=halo_s.at[i], recv_sem=halo_r.at[i], device_id=place, device_id_type=MESH,
        )

    span_r = {-1: (top, rows + top, HALO), 0: (top, top, rows), 1: (top + rows - HALO, 0, HALO)}
    span_c = {-1: (left, left + width, SIDE), 0: (left, left, width), 1: (left + width - SIDE, 0, SIDE)}

    def x_routes():
        i = 0
        routes = {-1: [], 0: [], 1: []}
        for dl, side in [(0, -1), (0, 1), (-1, 0), (-1, -1), (-1, 1), (1, 0), (1, -1), (1, 1)]:
            sr, dr, nr = span_r[dl]
            sc, dc, nc = span_c[side]
            routes[dl].append(remote(X, at(dl, side), sr, dr, nr, sc, dc, nc, i))
            i += 1
        return routes

    def g_routes():
        i = 8
        routes = {-1: [], 0: [], 1: []}
        out_src = left + ch * (width - SIDE)
        out_dst = other * (left + width)
        for dl in (0, -1, 1):
            sr, dr, nr = span_r[dl]
            if dl:
                routes[dl].append(remote(G, at(dl, 0), sr, dr, nr, other * SIDE, other * SIDE, reach, i))
                i += 1
            routes[dl].append(remote(G, outward(dl), sr, dr, nr, out_src, out_dst, SIDE, i))
            i += 1
        return routes

    def halo_start(routes, order):
        for dl in order:
            def go(dl=dl):
                for copy in routes[dl]:
                    copy.start()

            guarded(dl, go)

    def halo_finish(routes, order):
        for dl in order:
            def sent(dl=dl):
                for copy in routes[dl]:
                    copy.wait_send()

            def got(dl=dl):
                for copy in routes[dl]:
                    copy.wait_recv()

            guarded(dl, sent)
            guarded(-dl, got)

    def clear_poles(buf):
        @pl.when(lat == 0)
        def _():
            buf[0:HALO] = jnp.zeros((HALO, pitch, chans), BF16)

        @pl.when(lat == n_lat - 1)
        def _():
            buf[rows + HALO : rows + 2 * HALO] = jnp.zeros((HALO, pitch, chans), BF16)

    clear_poles(X)
    clear_poles(G)

    reshard.wait()
    for r in range(rows):
        X[top + r, left : left + width] = (
            jnp.concatenate([both[0, r], both[1, r]], axis=0).astype(F32).T.astype(BF16)
        )
    x_halo = x_routes()
    halo_start(x_halo, (-1, 1, 0))

    def pay_copies(peer):
        return [
            pltpu.make_async_remote_copy(
                src_ref=src.at[peer], dst_ref=dst, send_sem=ss.at[peer], recv_sem=rs.at[lat],
                device_id={"lat": peer}, device_id_type=MESH,
            )
            for src, dst, ss, rs in [
                (pay_at, R_at.at[lat], at_ss, at_rs), (pay_p, R_p.at[lat], p_ss, p_rs),
                (pay, R.at[lat, ch], pay_ss, pay_rs),
            ]
        ]

    def arrival(kind, peer):
        src, dst, ss, rs = [
            (pay_at.at[peer], R_at.at[peer], at_ss, at_rs), (pay_p.at[peer], R_p.at[peer], p_ss, p_rs),
            (pay.at[peer], R.at[peer, ch], pay_ss, pay_rs),
        ][kind]
        return pltpu.make_async_remote_copy(
            src_ref=src, dst_ref=dst, send_sem=ss.at[peer], recv_sem=rs.at[peer],
            device_id={"lat": peer}, device_id_type=MESH,
        )

    def start_pay(j, near):
        peer = peer_of(j)
        is_near = (peer == lat + 1) | (peer == lat - 1)

        @pl.when(is_near if near else jnp.logical_not(is_near))
        def _():
            for copy in pay_copies(peer):
                copy.start()

    each(min(2, n_lat - 1), lambda j: start_pay(j, True))

    @pl.when(lat >= 2)
    def _():
        pl.semaphore_wait(heard_up, 1)

        @pl.when(has_down)
        def _():
            tell(heard_up, 1)

    @pl.when(lat <= n_lat - 3)
    def _():
        pl.semaphore_wait(heard_down, 1)

        @pl.when(has_up)
        def _():
            tell(heard_down, -1)

    each(n_lat - 1, lambda j: start_pay(j, False))

    R[lat, ch] = pay[lat]
    R_at[lat] = pay_at[lat]
    R_p[lat] = pay_p[lat]

    def forward(t):
        return pltpu.make_async_remote_copy(
            src_ref=R.at[t, ch], dst_ref=R.at[t, ch], send_sem=fwd_s.at[t], recv_sem=fwd_r.at[t],
            device_id=sibling, device_id_type=MESH,
        )

    forward(lat).start()
    for load in loads[4:]:
        load.wait()
    for kind, k in enumerate((kin, kout, kout, kin)):
        for a in range(3):
            for b in range(3):
                tap = k[a, b].astype(F32).T.astype(BF16) if kind < 2 else k[2 - a, 2 - b]
                kw[kind, a, b * chans : (b + 1) * chans] = tap
    Z[...] = jnp.zeros(Z.shape, F32)

    def hidden_rows(r0, count):
        acc = conv(X3, 0, r0, count) + bias[...]
        s = sigmoid(acc)
        slope[r0 * pitch : (r0 + count) * pitch, :] = s * (1.0 + acc * (1.0 - s))
        h = acc * s
        for i in range(count):
            row = h[i * pitch : (i + 1) * pitch]
            f = edge_factor(r0 + i)
            if f is not None:
                row = row * f
            put_row(H3, r0 + i, row.astype(BF16).astype(F32))

    halo_finish(x_halo, (0,))
    for r in range(top, top + rows):
        put_row(X3, r, X[r].astype(F32))
    for r0 in range(HALO, rows, 2):
        hidden_rows(r0, 2)
    halo_finish(x_halo, (-1, 1))
    for r in (0, 1, top + rows, top + rows + 1):
        put_row(X3, r, X[r].astype(F32))
    hidden_rows(0, HALO)
    hidden_rows(rows, HALO)

    swaps = []
    for r0 in range(0, rows, WIDE):
        acc = conv(H3, 1, r0, WIDE)
        for i in range(WIDE):
            r = r0 + i
            state = X[top + r, left : left + width].astype(F32)
            den = (state + acc[i * pitch + left : i * pitch + left + width]).astype(BF16)
            den_s[r] = den
            wide = den.astype(F32)
            base[r * width : (r + 1) * width, :] = keep_rate * state + blend_rate * wide
            DF[pl.ds(pl.multiple_of(r * cols + ch * width, width), width), :] = wide
        part = pl.ds(r0, WIDE)
        swaps.append(pair_copy(den_s.at[part], den_r.at[part], 1 + r0 // WIDE))
        swaps[-1].start()

    def local_copy(t):
        return pltpu.make_async_copy(R_at.at[t], at_s.at[t], copy_sem.at[t])

    def take_small(j):
        peer = peer_of(j)
        for kind in (0, 1):
            arrival(kind, peer).wait()
        local_copy(peer).start()

    local_copy(lat).start()
    each(n_lat - 1, take_small)

    def take_pay(j):
        peer = peer_of(j)
        arrival(2, peer).wait()
        forward(peer).start()

    each(n_lat - 1, take_pay)
    for i, swap in enumerate(swaps):
        swap.wait()
        for r in range(i * WIDE, (i + 1) * WIDE):
            DF[pl.ds(pl.multiple_of(r * cols + other * width, width), width), :] = den_r[r].astype(F32)
    each(n_lat, lambda t: local_copy(t).wait())

    start = ch * (cols - reach)

    def source_of(j):
        return jnp.where(j == 0, lat, peer_of(jnp.maximum(j - 1, 0)))

    def observe(g, first):
        owners = [source_of(g * sources + i) for i in range(sources)]
        for t in owners:
            forward(t).wait()
        for i in range(GROUP):
            t, k = owners[i // CAP], i % CAP
            r0 = at_s[t, 2 * k, 0]
            q0 = at_s[t, 2 * k + 1, 0]
            w = jnp.concatenate([R[t, 0, k, 0:half], R[t, 1, k, 0:half]], axis=0)
            val = jnp.concatenate([R[t, 0, k, half:chans], R[t, 1, k, half:chans]], axis=0)
            prec = jnp.broadcast_to(R_p[t, k : k + 1, :], (chans, obs)).T
            patch = jnp.concatenate(
                [DF[pl.ds((r0 + a) * cols + q0, PW), :] for a in range(PH)], axis=0
            ).astype(BF16)
            predicted = jnp.dot(w, patch, preferred_element_type=F32)
            residual = predicted - val.astype(F32).T
            res_t[t, k] = residual
            weighted = (residual * prec).astype(BF16)
            pulled = jnp.dot(w.T, weighted, preferred_element_type=F32)
            for a in range(PH):
                Z[pl.ds((i * PH + a) * strip + reach, PW), :] = pulled[a * PW : (a + 1) * PW]
        for r in (0, 1, rows - 2, rows - 1, *range(2, rows - 2)):
            total = None
            for i in range(GROUP):
                t, k = owners[i // CAP], i % CAP
                r0 = at_s[t, 2 * k, 0]
                place = jnp.clip(at_s[t, 2 * k + 1, 0] - start, -PW, reach)
                inside = (r >= r0) & (r < r0 + PH)
                begin = jnp.where(inside, (i * PH + r - r0) * strip + reach - place, blank)
                v = Z[pl.ds(begin, reach), :]
                total = v if total is None else total + v
            span_w = pl.ds(pl.multiple_of(r * pitch + other * SIDE, SIDE), reach)
            if not first:
                total = total + GW[span_w, :]
            GW[span_w, :] = total
            G[top + r, pl.ds(pl.multiple_of(other * SIDE, SIDE), reach)] = total.astype(BF16)

    observe(0, True)
    if slots != GROUP:
        lax.fori_loop(1, slots // GROUP, lambda g, _: observe(g, False) or 0, 0)
    g_halo = g_routes()
    halo_start(g_halo, (-1, 1, 0))

    def turn(t):
        for k in range(CAP):
            res = res_t[t, k].T
            inn[t, k] = jnp.where(ch == 0, res[0:half], res[half:chans]).astype(BF16)

    each(n_lat, turn)

    def inn_copy(peer, landing):
        return pltpu.make_async_remote_copy(
            src_ref=inn.at[peer], dst_ref=inn_r.at[landing],
            send_sem=inn_ss.at[peer], recv_sem=inn_rs.at[landing],
            device_id={"lat": peer}, device_id_type=MESH,
        )

    each(n_lat - 1, lambda j: inn_copy(peer_of(j), lat).start())
    inn_r[lat] = inn[lat]

    def grad_rows(r0, count):
        g = conv(X3, 2, r0, count) * slope[r0 * pitch : (r0 + count) * pitch, :]
        for i in range(count):
            row = g[i * pitch : (i + 1) * pitch]
            f = edge_factor(r0 + i)
            if f is not None:
                row = row * f
            put_row(H3, r0 + i, row.astype(BF16).astype(F32))

    halo_finish(g_halo, (0,))
    for r in range(top, top + rows):
        put_row(X3, r, G[r].astype(F32))
    for r0 in range(HALO, rows, 2):
        grad_rows(r0, 2)
    halo_finish(g_halo, (-1, 1))
    for r in (0, 1, top + rows, top + rows + 1):
        put_row(X3, r, G[r].astype(F32))
    grad_rows(0, HALO)
    grad_rows(rows, HALO)

    mine = pl.ds(pl.multiple_of(ch * width, width), width)
    theirs = pl.ds(pl.multiple_of(other * width, width), width)
    back_home = []
    for r0 in range(0, rows, WIDE):
        acc = conv(H3, 3, r0, WIDE)
        for i in range(WIDE):
            r = r0 + i
            grad = GW[r * pitch + left : r * pitch + left + width, :] + acc[i * pitch + left : i * pitch + left + width]
            res = (base[r * width : (r + 1) * width, :] - guide_rate * grad).T
            out_h[0, pl.ds(r, half, stride=rows), :] = jnp.where(ch == 0, res[0:half], res[half:chans])
            out_s[r] = jnp.where(ch == 0, res[half:chans], res[0:half]).astype(BF16)
        sent = pl.ds(r0, WIDE)
        back_home.append(pair_copy(out_s.at[sent], out_r.at[sent], 1 + (rows + r0) // WIDE))
        back_home[-1].start()
    out[:, mine] = out_h[0]

    def take_inn(j):
        peer = peer_of(j)
        inn_copy(peer, peer).wait()

    each(n_lat - 1, take_inn)

    def fetch(b, _):
        slot = plan[b]
        inn_out[b] = inn_r[slot // CAP, slot % CAP]
        return 0

    lax.fori_loop(0, blocks, fetch, 0)
    for i, copy in enumerate(back_home):
        copy.wait()
        for r in range(i * WIDE, (i + 1) * WIDE):
            out_h[1, pl.ds(r, half, stride=rows), :] = out_r[r].astype(F32)
    out[:, theirs] = out_h[1]


def body(n_lat, n_lon, noisy_state, kernel_in, bias_in, kernel_out, interp_weight, observed,
         obs_precision, dest_tile, row_offset, col_offset):
    half, rows, cols = noisy_state.shape
    chans = 2 * half
    width = cols // 2
    blocks, obs, cells = interp_weight.shape
    slots = n_lat * CAP
    pitch = width + 2 * SIDE
    reach = width + SIDE
    px = rows * width
    pairs = 1 + 2 * (rows // WIDE)
    vmem = pl.BlockSpec(memory_space=pltpu.VMEM)
    hbm = pl.BlockSpec(memory_space=pltpu.HBM)
    smem = pl.BlockSpec(memory_space=pltpu.SMEM)
    dma = pltpu.SemaphoreType.DMA
    call = pl.pallas_call(
        functools.partial(kernel, n_lat, n_lon, rows, width, half, blocks),
        out_shape=(
            pltpu.VMEM((half * rows, cols), F32),
            pltpu.VMEM((blocks, half, obs), BF16),
        ),
        in_specs=[smem] * 3 + [hbm] * 3 + [vmem] + [hbm] * 3,
        out_specs=(vmem, vmem),
        scratch_shapes=[
            pltpu.VMEM((half, rows, cols), BF16),
            pltpu.VMEM((2, half * rows, width), F32),
            pltpu.VMEM((rows, half, width), BF16),
            pltpu.VMEM(kernel_in.shape, BF16),
            pltpu.VMEM(kernel_out.shape, BF16),
            pltpu.VMEM(interp_weight.shape, BF16),
            pltpu.VMEM(observed.shape, BF16),
            pltpu.VMEM(obs_precision.shape, BF16),
            pltpu.VMEM(obs_precision.shape, F32),
            pltpu.VMEM((4, 3, 3 * chans, chans), BF16),
            dma((6,)),
            pltpu.VMEM((2, rows, half, width), BF16),
            pltpu.VMEM((rows + 4, pitch, chans), BF16),
            pltpu.VMEM(((rows + 4) * pitch, 3 * chans), BF16),
            pltpu.VMEM(((rows + 2) * pitch, 3 * chans), BF16),
            pltpu.VMEM(((rows + 2) * pitch, chans), F32),
            pltpu.VMEM((px, chans), F32),
            pltpu.VMEM((rows * cols, chans), F32),
            pltpu.VMEM((rows, width, chans), BF16),
            pltpu.VMEM((rows, width, chans), BF16),
            pltpu.VMEM((n_lat, CAP, chans, obs), BF16),
            pltpu.VMEM((n_lat, SMALL, obs), I32),
            pltpu.VMEM((n_lat, SMALL, obs), F32),
            pltpu.VMEM((n_lat, 2, CAP, chans, obs), BF16),
            pltpu.VMEM((n_lat, SMALL, obs), I32),
            pltpu.VMEM((n_lat, SMALL, obs), F32),
            pltpu.SMEM((n_lat, SMALL, obs), I32),
            pltpu.VMEM((n_lat, CAP, obs, chans), F32),
            pltpu.VMEM((GROUP * PH * (2 * reach + PW) + reach, chans), F32),
            pltpu.VMEM((rows + 4, pitch, chans), BF16),
            pltpu.VMEM((rows * pitch, chans), F32),
            pltpu.VMEM((n_lat, CAP, half, obs), BF16),
            pltpu.VMEM((n_lat, CAP, half, obs), BF16),
            pltpu.VMEM((2, half * rows, width), F32),
            pltpu.VMEM((rows, half, width), BF16),
            pltpu.VMEM((rows, half, width), BF16),
            pltpu.SMEM((blocks,), I32),
            pltpu.SemaphoreType.REGULAR,
            pltpu.SemaphoreType.REGULAR,
            dma((13,)), dma((13,)),
            dma((pairs,)), dma((pairs,)),
            dma((n_lat,)), dma((n_lat,)),
            dma((n_lat,)), dma((n_lat,)),
            dma((n_lat,)), dma((n_lat,)),
            dma((n_lat,)), dma((n_lat,)),
            dma((n_lat,)),
            dma((n_lat,)), dma((n_lat,)),
        ],
        compiler_params=pltpu.CompilerParams(
            collective_id=0, has_side_effects=True, vmem_limit_bytes=(63 if slots <= GROUP else 48) * 1024 * 1024
        ),
    )
    out, innovation = call(
        dest_tile, row_offset, col_offset, noisy_state, kernel_in, kernel_out,
        bias_in.reshape(1, chans), interp_weight, observed, obs_precision,
    )
    return out.reshape(half, rows, cols), innovation


def solution(mesh):
    return jax.shard_map(
        functools.partial(body, mesh.shape["lat"], mesh.shape["lon"]),
        mesh=mesh,
        in_specs=(
            P(("grp", "ch"), "lat", "lon"),
            P(),
            P(),
            P(),
            P(("grp", "lat", "lon"), None, None),
            P(("grp", "lat", "lon"), "ch", None),
            P(("grp", "lat", "lon"), None),
            P(("grp", "lat", "lon")),
            P(("grp", "lat", "lon")),
            P(("grp", "lat", "lon")),
        ),
        out_specs=(P(("grp", "ch"), "lat", "lon"), P(("grp", "lat", "lon"), "ch", None)),
        check_vma=False,
    )
```

time: 31.1 us -> 28.9 us (0.929)
  Pallas kernels: 28.9 us -> 26.7 us
    pallas_call x1, Pallas kernels: 28.9 us -> 26.7 us  [body(): call(dest_tile, row_offset, col_offset, noisy_state, kernel_in, kernel_ou...]
where the time goes in v2:
time: 28.9 us; the launch traced here: 28.7 us
  Pallas kernels  26.7 us (92%)
  local copies, waits for them, and re-layouts  1.42 us (5%)
  between operations  0.64 us (2%)
    pallas_call x1, Pallas kernels, body(): call(dest_tile, row_offset, col_offset, noisy_state, kernel_in, kernel_ou...  26.7 us
    unnamed x2, local copies, waits for them, and re-layouts  1.42 us

profile of v2, /device:TPU:0, one launch (start us, length us, event | category | flops | bytes accessed | tf_op | source)
XLA Modules:
  0.0 28.7 jit_solution(11499509780924783945)
XLA Ops:
  0.6 26.7 %shard_map.113 = (f32[512,256]{1,0:T(8,128)S(1)}, bf16[4,64,128]{2,1,0:T(8,128)(2,1)S(1)}) custom-call(s32[4]{0:T(128)} %dest.1, s32[4]{0:T(128)} %row_off.1, s32[4]{0:T(128)} %col_off.1, bf16[64,8,256]{2,1,0:T(8,128)(2,1)} %x_hbm.1, bf16[3,3,128,128]{3,2,1,0:T(8,128)(2,1)} %kin_hbm.1, bf16[3,3,128,128]{3,2,1,0:T(8,128)(2,1)} %kout_hbm.1, f32[1,128]{1,0:T(1,128)} %bitcast.3, ...), custom_call_target="tpu_custom_call" | custom-call | tf_op jit(solution)/shard_map/pallas_call | solution.py:621
  27.3 0.8 %copy.14 = f32[64,8,256]{2,1,0:T(8,128)} copy(f32[64,8,256]{2,1,0:T(8,128)S(1)} %bitcast.2) | data formatting | bytes 1048576
  28.1 0.6 %copy.15 = bf16[4,64,128]{2,1,0:T(8,128)(2,1)} copy(bf16[4,64,128]{2,1,0:T(8,128)(2,1)S(1)} %get-tuple-element.7) | data formatting | bytes 131072

commit v3 on v2

--- a/solution.py
+++ b/solution.py
@@ -43,10 +43,10 @@
     dest, row_off, col_off, x_hbm, kin_hbm, kout_hbm, bias, weight_hbm, values_hbm, scale_hbm,
     out, inn_out,
     xv, xs, x_send, kin, kout, weight, values, scale_raw, scale, kw, load_sem,
-    both, X, X3, H3, slope, base, DF, den_s, den_r, pay, pay_at, pay_p, R, R_at, R_p, at_s,
-    res_t, Z, G, GW, inn, inn_r, out_h, out_s, out_r,
+    both, X, X3, H3, slope, base, DF, den_s, den_r, block_a, block_b, block_d,
+    pay, pay_at, pay_p, R, R_at, R_p, at_s, patches, pat_s, pat_r, Z, G, GW, out_h, out_s, out_r,
     plan, heard_up, heard_down,
-    halo_s, halo_r, pair_s, pair_r, pay_ss, pay_rs, at_ss, at_rs, p_ss, p_rs, fwd_s, fwd_r, copy_sem, inn_ss, inn_rs,
+    halo_s, halo_r, pair_s, pair_r, pay_ss, pay_rs, at_ss, at_rs, p_ss, p_rs, fwd_s, fwd_r, copy_sem, pat_ss, pat_rs,
 ):
     lat, lon, ch = lax.axis_index("lat"), lax.axis_index("lon"), lax.axis_index("ch")
     other = 1 - ch
@@ -126,25 +126,40 @@
     if blocks > 8:
         lax.fori_loop(0, blocks, count_block, 0)
 
-    def w_half(w):
-        return jnp.where(ch == 0, w[0:half].astype(F32), w[half:chans].astype(F32)).astype(BF16)
-
-    def pack_slot(s, _):
+    quarter = half // 2
+    packed = quarter + half
+
+    def corner():
+        return (
+            lax.broadcasted_iota(I32, (half, cells), 0), lax.broadcasted_iota(I32, (half, cells), 1)
+        )
+
+    def prepare(b):
+        row, lane = corner()
+        w = weight[b]
+        p = scale[pl.ds(b, 1), :]
+        normal = jnp.dot((w.astype(F32).T * p).astype(BF16), w, preferred_element_type=F32)
+        low = normal[half:cells]
+        tri = jnp.where((lane < half) & (lane > row), pltpu.roll(low, half, 1), normal[0:half])
+        tri = jnp.where(lane == row, 0.5 * tri, tri)
+        block_a[b] = jnp.where(ch == 0, tri[0:quarter], tri[quarter:half])
+        block_d[pl.ds(b, 1), :] = jnp.sum(jnp.where(lane == row + half, 0.5 * low, 0.0), axis=0, keepdims=True)
+        block_b[b] = jnp.dot((values[b].astype(F32) * p).astype(BF16), w, preferred_element_type=F32)
+
+    def pack_slot(s):
         def look(b, found):
             return jnp.where(plan[b] == s, b, found)
 
-        found = lax.fori_loop(0, blocks, look, -1)
+        found = lax.fori_loop(0, blocks, look, -1, unroll=blocks <= 8)
         source = jnp.maximum(found, 0)
         fill = jnp.where(found >= 0, 1.0, 0.0)
-        w = (weight[source].astype(F32) * fill).astype(BF16)
         t = s // CAP
         k = s % CAP
-        pay[t, k, 0:half] = w_half(w)
-        pay[t, k, half:chans] = values[source]
-        pay_p[t, pl.ds(k, 1), :] = scale[pl.ds(source, 1), :]
+        pay[t, k, 0:quarter] = (block_a[source] * fill).astype(BF16)
+        pay[t, k, quarter:packed] = (block_b[source] * fill).astype(BF16)
+        pay_p[t, pl.ds(k, 1), :] = block_d[pl.ds(source, 1), :] * fill
         pay_at[t, pl.ds(2 * k, 1), :] = jnp.full((1, obs), row_off[source], I32)
         pay_at[t, pl.ds(2 * k + 1, 1), :] = jnp.full((1, obs), col_off[source], I32)
-        return 0
 
     loads[0].wait()
     for h in range(2):
@@ -182,7 +197,40 @@
     scale[...] = scale_raw[...].astype(F32)
     pay_at[...] = jnp.zeros(pay_at.shape, I32)
     pay_p[...] = jnp.zeros(pay_p.shape, F32)
-    lax.fori_loop(0, slots, pack_slot, 0)
+    each(blocks, prepare)
+    each(slots, pack_slot)
+    def pay_copies(peer, kinds):
+        return [
+            pltpu.make_async_remote_copy(
+                src_ref=src.at[peer], dst_ref=dst, send_sem=ss.at[peer], recv_sem=rs.at[lat],
+                device_id={"lat": peer}, device_id_type=MESH,
+            )
+            for src, dst, ss, rs in (
+                (pay_at, R_at.at[lat], at_ss, at_rs), (pay_p, R_p.at[lat], p_ss, p_rs),
+                (pay, R.at[lat, ch], pay_ss, pay_rs),
+            )[kinds]
+        ]
+
+    def arrival(kind, peer):
+        src, dst, ss, rs = [
+            (pay_at.at[peer], R_at.at[peer], at_ss, at_rs), (pay_p.at[peer], R_p.at[peer], p_ss, p_rs),
+            (pay.at[peer], R.at[peer, ch], pay_ss, pay_rs),
+        ][kind]
+        return pltpu.make_async_remote_copy(
+            src_ref=src, dst_ref=dst, send_sem=ss.at[peer], recv_sem=rs.at[peer],
+            device_id={"lat": peer}, device_id_type=MESH,
+        )
+
+    def start_pay(j, near, kinds=slice(0, 3)):
+        peer = peer_of(j)
+        is_near = (peer == lat + 1) | (peer == lat - 1)
+
+        @pl.when(is_near if near else jnp.logical_not(is_near))
+        def _():
+            for copy in pay_copies(peer, kinds):
+                copy.start()
+
+    each(min(2, n_lat - 1), lambda j: start_pay(j, True))
 
     def put_row(taps, r, v):
         taps[r * pitch : (r + 1) * pitch, 0:chans] = pltpu.roll(v, 1, 0).astype(BF16)
@@ -289,39 +337,6 @@
     x_halo = x_routes()
     halo_start(x_halo, (-1, 1, 0))
 
-    def pay_copies(peer):
-        return [
-            pltpu.make_async_remote_copy(
-                src_ref=src.at[peer], dst_ref=dst, send_sem=ss.at[peer], recv_sem=rs.at[lat],
-                device_id={"lat": peer}, device_id_type=MESH,
-            )
-            for src, dst, ss, rs in [
-                (pay_at, R_at.at[lat], at_ss, at_rs), (pay_p, R_p.at[lat], p_ss, p_rs),
-                (pay, R.at[lat, ch], pay_ss, pay_rs),
-            ]
-        ]
-
-    def arrival(kind, peer):
-        src, dst, ss, rs = [
-            (pay_at.at[peer], R_at.at[peer], at_ss, at_rs), (pay_p.at[peer], R_p.at[peer], p_ss, p_rs),
-            (pay.at[peer], R.at[peer, ch], pay_ss, pay_rs),
-        ][kind]
-        return pltpu.make_async_remote_copy(
-            src_ref=src, dst_ref=dst, send_sem=ss.at[peer], recv_sem=rs.at[peer],
-            device_id={"lat": peer}, device_id_type=MESH,
-        )
-
-    def start_pay(j, near):
-        peer = peer_of(j)
-        is_near = (peer == lat + 1) | (peer == lat - 1)
-
-        @pl.when(is_near if near else jnp.logical_not(is_near))
-        def _():
-            for copy in pay_copies(peer):
-                copy.start()
-
-    each(min(2, n_lat - 1), lambda j: start_pay(j, True))
-
     @pl.when(lat >= 2)
     def _():
         pl.semaphore_wait(heard_up, 1)
@@ -338,7 +353,8 @@
         def _():
             tell(heard_down, -1)
 
-    each(n_lat - 1, lambda j: start_pay(j, False))
+    each(n_lat - 1, lambda j: start_pay(j, False, slice(0, 2)))
+    each(n_lat - 1, lambda j: start_pay(j, False, slice(2, 3)))
 
     R[lat, ch] = pay[lat]
     R_at[lat] = pay_at[lat]
@@ -377,16 +393,11 @@
         put_row(X3, r, X[r].astype(F32))
     for r0 in range(HALO, rows, 2):
         hidden_rows(r0, 2)
-    halo_finish(x_halo, (-1, 1))
-    for r in (0, 1, top + rows, top + rows + 1):
-        put_row(X3, r, X[r].astype(F32))
-    hidden_rows(0, HALO)
-    hidden_rows(rows, HALO)
-
     swaps = []
-    for r0 in range(0, rows, WIDE):
-        acc = conv(H3, 1, r0, WIDE)
-        for i in range(WIDE):
+
+    def denoise_rows(r0, count):
+        acc = conv(H3, 1, r0, count)
+        for i in range(count):
             r = r0 + i
             state = X[top + r, left : left + width].astype(F32)
             den = (state + acc[i * pitch + left : i * pitch + left + width]).astype(BF16)
@@ -394,34 +405,71 @@
             wide = den.astype(F32)
             base[r * width : (r + 1) * width, :] = keep_rate * state + blend_rate * wide
             DF[pl.ds(pl.multiple_of(r * cols + ch * width, width), width), :] = wide
-        part = pl.ds(r0, WIDE)
-        swaps.append(pair_copy(den_s.at[part], den_r.at[part], 1 + r0 // WIDE))
-        swaps[-1].start()
+        part = pl.ds(r0, count)
+        swaps.append((r0, count, pair_copy(den_s.at[part], den_r.at[part], 1 + len(swaps))))
+        swaps[-1][2].start()
+
+    inner = [(r0, min(WIDE, rows - HALO - r0)) for r0 in range(HALO, rows - HALO, WIDE)]
+    outer = [(0, HALO), (rows - HALO, HALO)]
+    for r0, count in inner:
+        denoise_rows(r0, count)
+    halo_finish(x_halo, (-1, 1))
+    for r in (0, 1, top + rows, top + rows + 1):
+        put_row(X3, r, X[r].astype(F32))
+    hidden_rows(0, HALO)
+    hidden_rows(rows, HALO)
+    for r0, count in outer:
+        denoise_rows(r0, count)
 
     def local_copy(t):
         return pltpu.make_async_copy(R_at.at[t], at_s.at[t], copy_sem.at[t])
 
-    def take_small(j):
+    def take_at(j):
         peer = peer_of(j)
-        for kind in (0, 1):
-            arrival(kind, peer).wait()
+        arrival(0, peer).wait()
         local_copy(peer).start()
 
     local_copy(lat).start()
-    each(n_lat - 1, take_small)
+    each(n_lat - 1, take_at)
 
     def take_pay(j):
         peer = peer_of(j)
-        arrival(2, peer).wait()
+        for kind in (1, 2):
+            arrival(kind, peer).wait()
         forward(peer).start()
 
     each(n_lat - 1, take_pay)
-    for i, swap in enumerate(swaps):
+    for r0, count, swap in swaps:
         swap.wait()
-        for r in range(i * WIDE, (i + 1) * WIDE):
+        for r in range(r0, r0 + count):
             DF[pl.ds(pl.multiple_of(r * cols + other * width, width), width), :] = den_r[r].astype(F32)
     each(n_lat, lambda t: local_copy(t).wait())
 
+    def gather(t):
+        lane = lax.broadcasted_iota(I32, (half, chans), 1)
+        for k in range(CAP):
+            r0 = at_s[t, 2 * k, 0]
+            q0 = at_s[t, 2 * k + 1, 0]
+            cut = [DF[pl.ds((r0 + a) * cols + q0, PW), :] for a in range(PH)]
+            first = jnp.concatenate(cut[: PH // 2], axis=0)
+            second = jnp.concatenate(cut[PH // 2 :], axis=0)
+            patches[t, k, 0:half] = first.astype(BF16)
+            patches[t, k, half:cells] = second.astype(BF16)
+            keep_first = jnp.where(ch == 0, first, pltpu.roll(first, half, 1))
+            keep_second = jnp.where(ch == 0, pltpu.roll(second, half, 1), second)
+            pat_s[t, k] = jnp.where(lane < half, keep_first, keep_second).astype(BF16)
+
+    each(n_lat, gather)
+
+    def patch_copy(peer, landing):
+        return pltpu.make_async_remote_copy(
+            src_ref=pat_s.at[peer], dst_ref=pat_r.at[landing],
+            send_sem=pat_ss.at[peer], recv_sem=pat_rs.at[landing],
+            device_id={"lat": peer}, device_id_type=MESH,
+        )
+
+    each(n_lat - 1, lambda j: patch_copy(peer_of(j), lat).start())
+    pat_r[lat] = pat_s[lat]
     start = ch * (cols - reach)
 
     def source_of(j):
@@ -433,19 +481,15 @@
             forward(t).wait()
         for i in range(GROUP):
             t, k = owners[i // CAP], i % CAP
-            r0 = at_s[t, 2 * k, 0]
-            q0 = at_s[t, 2 * k + 1, 0]
-            w = jnp.concatenate([R[t, 0, k, 0:half], R[t, 1, k, 0:half]], axis=0)
-            val = jnp.concatenate([R[t, 0, k, half:chans], R[t, 1, k, half:chans]], axis=0)
-            prec = jnp.broadcast_to(R_p[t, k : k + 1, :], (chans, obs)).T
-            patch = jnp.concatenate(
-                [DF[pl.ds((r0 + a) * cols + q0, PW), :] for a in range(PH)], axis=0
-            ).astype(BF16)
-            predicted = jnp.dot(w, patch, preferred_element_type=F32)
-            residual = predicted - val.astype(F32).T
-            res_t[t, k] = residual
-            weighted = (residual * prec).astype(BF16)
-            pulled = jnp.dot(w.T, weighted, preferred_element_type=F32)
+            row, lane = corner()
+            tri = jnp.concatenate([R[t, 0, k, 0:quarter], R[t, 1, k, 0:quarter]], axis=0).astype(F32)
+            upper = jnp.where((lane <= row) | (lane >= half), tri, 0.0)
+            lower = jnp.where(lane > row + half, pltpu.roll(tri, half, 1), 0.0)
+            lower = jnp.where(lane == row + half, R_p[t, k : k + 1, :], lower)
+            side = jnp.concatenate([upper, lower], axis=0).astype(BF16)
+            normal = side + side.T
+            pull = jnp.concatenate([R[t, 0, k, quarter:packed], R[t, 1, k, quarter:packed]], axis=0)
+            pulled = jnp.dot(normal, patches[t, k], preferred_element_type=F32) - pull.astype(F32).T
             for a in range(PH):
                 Z[pl.ds((i * PH + a) * strip + reach, PW), :] = pulled[a * PW : (a + 1) * PW]
         for r in (0, 1, rows - 2, rows - 1, *range(2, rows - 2)):
@@ -470,23 +514,6 @@
     g_halo = g_routes()
     halo_start(g_halo, (-1, 1, 0))
 
-    def turn(t):
-        for k in range(CAP):
-            res = res_t[t, k].T
-            inn[t, k] = jnp.where(ch == 0, res[0:half], res[half:chans]).astype(BF16)
-
-    each(n_lat, turn)
-
-    def inn_copy(peer, landing):
-        return pltpu.make_async_remote_copy(
-            src_ref=inn.at[peer], dst_ref=inn_r.at[landing],
-            send_sem=inn_ss.at[peer], recv_sem=inn_rs.at[landing],
-            device_id={"lat": peer}, device_id_type=MESH,
-        )
-
-    each(n_lat - 1, lambda j: inn_copy(peer_of(j), lat).start())
-    inn_r[lat] = inn[lat]
-
     def grad_rows(r0, count):
         g = conv(X3, 2, r0, count) * slope[r0 * pitch : (r0 + count) * pitch, :]
         for i in range(count):
@@ -501,45 +528,59 @@
         put_row(X3, r, G[r].astype(F32))
     for r0 in range(HALO, rows, 2):
         grad_rows(r0, 2)
+    back_home = []
+
+    def finish_rows(r0, count):
+        acc = conv(H3, 3, r0, count)
+        for i in range(count):
+            r = r0 + i
+            grad = GW[r * pitch + left : r * pitch + left + width, :] + acc[i * pitch + left : i * pitch + left + width]
+            res = (base[r * width : (r + 1) * width, :] - guide_rate * grad).T
+            out_s[r] = jnp.where(ch == 0, res[half:chans], res[0:half]).astype(BF16)
+            out_h[0, pl.ds(r, half, stride=rows), :] = jnp.where(ch == 0, res[0:half], res[half:chans])
+        part = pl.ds(r0, count)
+        back_home.append((r0, count, pair_copy(out_s.at[part], out_r.at[part], 1 + len(swaps) + len(back_home))))
+        back_home[-1][2].start()
+
+    for r0, count in inner:
+        finish_rows(r0, count)
+    each(n_lat - 1, lambda j: patch_copy(peer_of(j), peer_of(j)).wait())
+
+    def innovate(b):
+        slot = plan[b]
+        part = pat_r[slot // CAP, slot % CAP].astype(F32)
+        patch = jnp.concatenate([part, pltpu.roll(part, half, 1)], axis=0).astype(BF16)
+        predicted = jnp.dot(weight[b], patch, preferred_element_type=F32).T
+        inn_out[b] = (predicted[0:half] - values[b].astype(F32)).astype(BF16)
+
+    each(blocks, innovate)
     halo_finish(g_halo, (-1, 1))
     for r in (0, 1, top + rows, top + rows + 1):
         put_row(X3, r, G[r].astype(F32))
     grad_rows(0, HALO)
     grad_rows(rows, HALO)
-
+    for r0, count in outer:
+        finish_rows(r0, count)
     mine = pl.ds(pl.multiple_of(ch * width, width), width)
     theirs = pl.ds(pl.multiple_of(other * width, width), width)
-    back_home = []
-    for r0 in range(0, rows, WIDE):
-        acc = conv(H3, 3, r0, WIDE)
-        for i in range(WIDE):
-            r = r0 + i
-            grad = GW[r * pitch + left : r * pitch + left + width, :] + acc[i * pitch + left : i * pitch + left + width]
-            res = (base[r * width : (r + 1) * width, :] - guide_rate * grad).T
-            out_h[0, pl.ds(r, half, stride=rows), :] = jnp.where(ch == 0, res[0:half], res[half:chans])
-            out_s[r] = jnp.where(ch == 0, res[half:chans], res[0:half]).astype(BF16)
-        sent = pl.ds(r0, WIDE)
-        back_home.append(pair_copy(out_s.at[sent], out_r.at[sent], 1 + (rows + r0) // WIDE))
-        back_home[-1].start()
     out[:, mine] = out_h[0]
 
-    def take_inn(j):
-        peer = peer_of(j)
-        inn_copy(peer, peer).wait()
-
-    each(n_lat - 1, take_inn)
-
-    def fetch(b, _):
-        slot = plan[b]
-        inn_out[b] = inn_r[slot // CAP, slot % CAP]
-        return 0
-
-    lax.fori_loop(0, blocks, fetch, 0)
-    for i, copy in enumerate(back_home):
+    for r0, count, copy in back_home:
         copy.wait()
-        for r in range(i * WIDE, (i + 1) * WIDE):
+        for r in range(r0, r0 + count):
             out_h[1, pl.ds(r, half, stride=rows), :] = out_r[r].astype(F32)
     out[:, theirs] = out_h[1]
+
+
+def store(out, innovation, out_hbm, innovation_hbm, sem):
+    copies = [
+        pltpu.make_async_copy(out, out_hbm, sem.at[0]),
+        pltpu.make_async_copy(innovation, innovation_hbm, sem.at[1]),
+    ]
+    for copy in copies:
+        copy.start()
+    for copy in copies:
+        copy.wait()
 
 
 def body(n_lat, n_lon, noisy_state, kernel_in, bias_in, kernel_out, interp_weight, observed,
@@ -552,7 +593,7 @@
     pitch = width + 2 * SIDE
     reach = width + SIDE
     px = rows * width
-    pairs = 1 + 2 * (rows // WIDE)
+    pairs = 1 + 2 * (2 - (HALO + HALO - rows) // WIDE)
     vmem = pl.BlockSpec(memory_space=pltpu.VMEM)
     hbm = pl.BlockSpec(memory_space=pltpu.HBM)
     smem = pl.BlockSpec(memory_space=pltpu.SMEM)
@@ -586,19 +627,22 @@
             pltpu.VMEM((rows * cols, chans), F32),
             pltpu.VMEM((rows, width, chans), BF16),
             pltpu.VMEM((rows, width, chans), BF16),
-            pltpu.VMEM((n_lat, CAP, chans, obs), BF16),
+            pltpu.VMEM((blocks, half // 2, cells), F32),
+            pltpu.VMEM((blocks, half, cells), F32),
+            pltpu.VMEM((blocks, cells), F32),
+            pltpu.VMEM((n_lat, CAP, half + half // 2, cells), BF16),
             pltpu.VMEM((n_lat, SMALL, obs), I32),
             pltpu.VMEM((n_lat, SMALL, obs), F32),
-            pltpu.VMEM((n_lat, 2, CAP, chans, obs), BF16),
+            pltpu.VMEM((n_lat, 2, CAP, half + half // 2, cells), BF16),
             pltpu.VMEM((n_lat, SMALL, obs), I32),
             pltpu.VMEM((n_lat, SMALL, obs), F32),
             pltpu.SMEM((n_lat, SMALL, obs), I32),
-            pltpu.VMEM((n_lat, CAP, obs, chans), F32),
+            pltpu.VMEM((n_lat, CAP, cells, chans), BF16),
+            pltpu.VMEM((n_lat, CAP, half, chans), BF16),
+            pltpu.VMEM((n_lat, CAP, half, chans), BF16),
             pltpu.VMEM((GROUP * PH * (2 * reach + PW) + reach, chans), F32),
             pltpu.VMEM((rows + 4, pitch, chans), BF16),
             pltpu.VMEM((rows * pitch, chans), F32),
-            pltpu.VMEM((n_lat, CAP, half, obs), BF16),
-            pltpu.VMEM((n_lat, CAP, half, obs), BF16),
             pltpu.VMEM((2, half * rows, width), F32),
             pltpu.VMEM((rows, half, width), BF16),
             pltpu.VMEM((rows, half, width), BF16),
@@ -622,6 +666,16 @@
         dest_tile, row_offset, col_offset, noisy_state, kernel_in, kernel_out,
         bias_in.reshape(1, chans), interp_weight, observed, obs_precision,
     )
+    out, innovation = pl.pallas_call(
+        store,
+        out_shape=(
+            jax.ShapeDtypeStruct((half * rows, cols), F32),
+            jax.ShapeDtypeStruct((blocks, half, obs), BF16),
+        ),
+        in_specs=[vmem, vmem],
+        out_specs=(hbm, hbm),
+        scratch_shapes=[dma((2,))],
+    )(*(pltpu.with_memory_space_constraint(a, pltpu.VMEM) for a in (out, innovation)))
     return out.reshape(half, rows, cols), innovation
 
 

time: 28.9 us -> 25.9 us (0.90)
  Pallas kernels: 26.7 us -> 25.1 us
  local copies, waits for them, and re-layouts: 1.42 us -> 0 us
    pallas_call x1, Pallas kernels: 26.7 us -> 24.3 us  [body(): call(dest_tile, row_offset, col_offset, noisy_state, kernel_in, kernel_ou...]
    unnamed x2 -> x0, local copies, waits for them, and re-layouts: 1.42 us -> none
    pallas_call x0 -> x1, Pallas kernels: none -> 0.82 us  [body(): pl.pallas_call(store, out_shape=(jax.ShapeDtypeStruct((half * rows, cols)...]
where the time goes in v3:
time: 25.9 us; the launch traced here: 25.8 us
  Pallas kernels  25.1 us (97%)
  between operations  0.64 us (2%)
    pallas_call x1, Pallas kernels, body(): call(dest_tile, row_offset, col_offset, noisy_state, kernel_in, kernel_ou...  24.3 us
    pallas_call x1, Pallas kernels, body(): pl.pallas_call(store, out_shape=(jax.ShapeDtypeStruct((half * rows, cols)...  0.82 us

profile of v3, /device:TPU:0, one launch (start us, length us, event | category | flops | bytes accessed | tf_op | source)
XLA Modules:
  0.0 25.8 jit_solution(14966947399696440609)
XLA Ops:
  0.6 24.3 %shard_map.113 = (f32[512,256]{1,0:T(8,128)S(1)}, bf16[4,64,128]{2,1,0:T(8,128)(2,1)S(1)}) custom-call(s32[4]{0:T(128)} %dest.1, s32[4]{0:T(128)} %row_off.1, s32[4]{0:T(128)} %col_off.1, bf16[64,8,256]{2,1,0:T(8,128)(2,1)} %x_hbm.1, bf16[3,3,128,128]{3,2,1,0:T(8,128)(2,1)} %kin_hbm.1, bf16[3,3,128,128]{3,2,1,0:T(8,128)(2,1)} %kout_hbm.1, f32[1,128]{1,0:T(1,128)} %bitcast.2, ...), custom_call_target="tpu_custom_call" | custom-call | tf_op jit(solution)/shard_map/pallas_call | solution.py:665
  24.9 0.8 %shard_map.114 = (f32[512,256]{1,0:T(8,128)}, bf16[4,64,128]{2,1,0:T(8,128)(2,1)}) custom-call(f32[512,256]{1,0:T(8,128)S(1)} %get-tuple-element.6.out, bf16[4,64,128]{2,1,0:T(8,128)(2,1)S(1)} %get-tuple-element.7.innovation), custom_call_target="tpu_custom_call" | custom-call | tf_op jit(solution)/shard_map/pallas_call | solution.py:669

commit v4 on v3

--- a/solution.py
+++ b/solution.py
@@ -12,7 +12,7 @@
 CAP = 2
 HALO = 2
 SIDE = 16
-GROUP = 8
+GROUP = 4
 WIDE = 4
 SMALL = 8
 
@@ -43,10 +43,10 @@
     dest, row_off, col_off, x_hbm, kin_hbm, kout_hbm, bias, weight_hbm, values_hbm, scale_hbm,
     out, inn_out,
     xv, xs, x_send, kin, kout, weight, values, scale_raw, scale, kw, load_sem,
-    both, X, X3, H3, slope, base, DF, den_s, den_r, block_a, block_b, block_d,
+    both, edge, edge_r, raw, edge_ss, edge_rs, raw_s, raw_r, X, X3, H3, slope, base, DF, den_s, den_r, block_a, block_b, block_d,
     pay, pay_at, pay_p, R, R_at, R_p, at_s, patches, pat_s, pat_r, Z, G, GW, out_h, out_s, out_r,
     plan, heard_up, heard_down,
-    halo_s, halo_r, pair_s, pair_r, pay_ss, pay_rs, at_ss, at_rs, p_ss, p_rs, fwd_s, fwd_r, copy_sem, pat_ss, pat_rs,
+    halo_s, halo_r, pair_s, pair_r, pay_ss, pay_rs, at_ss, at_rs, p_ss, p_rs, fwd_s, fwd_r, fat_s, fat_r, fp_s, fp_r, copy_sem, pat_ss, pat_rs,
 ):
     lat, lon, ch = lax.axis_index("lat"), lax.axis_index("lon"), lax.axis_index("ch")
     other = 1 - ch
@@ -100,6 +100,10 @@
 
     greet(at(0, -1))
     greet(at(0, 1))
+    chip_left = lax.rem(lon + n_lon - 1, n_lon)
+    chip_right = lax.rem(lon + 1, n_lon)
+    greet({"lon": chip_left})
+    greet({"lon": chip_right})
 
     @pl.when(has_up)
     def _():
@@ -125,9 +129,6 @@
         plan[b] = dest[b] * CAP + rank
     if blocks > 8:
         lax.fori_loop(0, blocks, count_block, 0)
-
-    quarter = half // 2
-    packed = quarter + half
 
     def corner():
         return (
@@ -142,7 +143,7 @@
         low = normal[half:cells]
         tri = jnp.where((lane < half) & (lane > row), pltpu.roll(low, half, 1), normal[0:half])
         tri = jnp.where(lane == row, 0.5 * tri, tri)
-        block_a[b] = jnp.where(ch == 0, tri[0:quarter], tri[quarter:half])
+        block_a[b] = tri
         block_d[pl.ds(b, 1), :] = jnp.sum(jnp.where(lane == row + half, 0.5 * low, 0.0), axis=0, keepdims=True)
         block_b[b] = jnp.dot((values[b].astype(F32) * p).astype(BF16), w, preferred_element_type=F32)
 
@@ -155,8 +156,8 @@
         fill = jnp.where(found >= 0, 1.0, 0.0)
         t = s // CAP
         k = s % CAP
-        pay[t, k, 0:quarter] = (block_a[source] * fill).astype(BF16)
-        pay[t, k, quarter:packed] = (block_b[source] * fill).astype(BF16)
+        pay[t, k, 0:half] = (block_b[source] * fill).astype(BF16)
+        pay[t, k, half:chans] = (block_a[source] * fill).astype(BF16)
         pay_p[t, pl.ds(k, 1), :] = block_d[pl.ds(source, 1), :] * fill
         pay_at[t, pl.ds(2 * k, 1), :] = jnp.full((1, obs), row_off[source], I32)
         pay_at[t, pl.ds(2 * k + 1, 1), :] = jnp.full((1, obs), col_off[source], I32)
@@ -168,10 +169,18 @@
     for r in range(rows):
         both[ch, r] = xs[ch, pl.ds(r, half, stride=rows), :].astype(BF16)
         x_send[r] = xs[other, pl.ds(r, half, stride=rows), :].astype(BF16)
+    lane = lax.broadcasted_iota(I32, (half, width), 1)
+    for n, (h, first) in enumerate(((0, True), (1, False), (1, True), (0, False))):
+        tile = None
+        for r in range(rows):
+            v = pltpu.roll(xs[h, pl.ds(r, half, stride=rows), :], (SIDE * r + (0 if first else SIDE)) % width, 1)
+            tile = v if tile is None else jnp.where(lane // SIDE == r, v, tile)
+        edge[n] = tile.astype(BF16)
+    edge_r[other, ch] = edge[2 + ch]
 
     tops = (lat + n_lat - 1) // n_lat
     bottoms = (2 * n_lat - 2 - lat) // n_lat
-    pl.semaphore_wait(barrier, 2 + 3 * tops + 3 * bottoms)
+    pl.semaphore_wait(barrier, 4 + 3 * tops + 3 * bottoms)
 
     def tell(sem, dlat):
         pl.semaphore_signal(sem, inc=1, device_id={"lat": lat + dlat}, device_id_type=MESH)
@@ -192,6 +201,49 @@
 
     reshard = pair_copy(x_send, both.at[ch], 0)
     reshard.start()
+
+    def raw_row(dl, mine):
+        row = 0 if dl < 0 else rows - HALO
+        src = both.at[ch, pl.ds(row, HALO)] if mine else x_send.at[pl.ds(row, HALO)]
+        side = 1 if dl < 0 else 0
+        return pltpu.make_async_remote_copy(
+            src_ref=src, dst_ref=raw.at[side, ch], send_sem=raw_s.at[2 * side + mine],
+            recv_sem=raw_r.at[2 * side + ch],
+            device_id={"lat": lat + dl, "ch": ch if mine else other}, device_id_type=MESH,
+        )
+
+    def raw_got(dl, c):
+        side = 0 if dl < 0 else 1
+        return pltpu.make_async_remote_copy(
+            src_ref=x_send.at[pl.ds(0, HALO)], dst_ref=raw.at[side, c], send_sem=raw_s.at[2 * side],
+            recv_sem=raw_r.at[2 * side + c], device_id={"lat": lat + dl}, device_id_type=MESH,
+        )
+
+    def edge_copy(n, src, side, place):
+        return pltpu.make_async_remote_copy(
+            src_ref=edge.at[src], dst_ref=edge_r.at[side, ch], send_sem=edge_ss.at[n],
+            recv_sem=edge_rs.at[2 * side + ch], device_id=place, device_id_type=MESH,
+        )
+
+    def edge_got(side, c):
+        return pltpu.make_async_remote_copy(
+            src_ref=edge.at[0], dst_ref=edge_r.at[side, c], send_sem=edge_ss.at[0],
+            recv_sem=edge_rs.at[2 * side + c], device_id=sibling, device_id_type=MESH,
+        )
+
+    for dl in (-1, 1):
+        @pl.when(has_up if dl < 0 else has_down)
+        def _(dl=dl):
+            raw_row(dl, 0).start()
+            raw_row(dl, 1).start()
+
+    edges = [
+        edge_copy(0, 0, 1, {"lon": chip_left, "ch": 1}),
+        edge_copy(1, 1, 0, {"lon": chip_right, "ch": 0}),
+        edge_copy(2, 3 - ch, ch, sibling),
+    ]
+    for copy in edges:
+        copy.start()
     for load in loads[1:4]:
         load.wait()
     scale[...] = scale_raw[...].astype(F32)
@@ -199,38 +251,47 @@
     pay_p[...] = jnp.zeros(pay_p.shape, F32)
     each(blocks, prepare)
     each(slots, pack_slot)
-    def pay_copies(peer, kinds):
-        return [
-            pltpu.make_async_remote_copy(
-                src_ref=src.at[peer], dst_ref=dst, send_sem=ss.at[peer], recv_sem=rs.at[lat],
-                device_id={"lat": peer}, device_id_type=MESH,
-            )
-            for src, dst, ss, rs in (
-                (pay_at, R_at.at[lat], at_ss, at_rs), (pay_p, R_p.at[lat], p_ss, p_rs),
-                (pay, R.at[lat, ch], pay_ss, pay_rs),
-            )[kinds]
-        ]
-
-    def arrival(kind, peer):
-        src, dst, ss, rs = [
-            (pay_at.at[peer], R_at.at[peer], at_ss, at_rs), (pay_p.at[peer], R_p.at[peer], p_ss, p_rs),
-            (pay.at[peer], R.at[peer, ch], pay_ss, pay_rs),
-        ][kind]
-        return pltpu.make_async_remote_copy(
-            src_ref=src, dst_ref=dst, send_sem=ss.at[peer], recv_sem=rs.at[peer],
+    def by_core(fn):
+        for c in (0, 1):
+            pl.when(ch == c)(functools.partial(fn, c))
+
+    def big(peer, landing, c):
+        part = pl.ds(0, half * (1 + c))
+        return pltpu.make_async_remote_copy(
+            src_ref=pay.at[peer, :, part], dst_ref=R.at[landing, c, :, part],
+            send_sem=pay_ss.at[peer], recv_sem=pay_rs.at[landing],
             device_id={"lat": peer}, device_id_type=MESH,
         )
 
-    def start_pay(j, near, kinds=slice(0, 3)):
-        peer = peer_of(j)
-        is_near = (peer == lat + 1) | (peer == lat - 1)
-
-        @pl.when(is_near if near else jnp.logical_not(is_near))
-        def _():
-            for copy in pay_copies(peer, kinds):
-                copy.start()
-
-    each(min(2, n_lat - 1), lambda j: start_pay(j, True))
+    def small(peer, landing, kind):
+        src, dst, ss, rs = ((pay_at, R_at, at_ss, at_rs), (pay_p, R_p, p_ss, p_rs))[kind]
+        return pltpu.make_async_remote_copy(
+            src_ref=src.at[peer], dst_ref=dst.at[landing], send_sem=ss.at[peer], recv_sem=rs.at[landing],
+            device_id={"lat": peer}, device_id_type=MESH,
+        )
+
+    def start_small(peer):
+        @pl.when(ch == 1)
+        def _():
+            small(peer, lat, 0).start()
+            small(peer, lat, 1).start()
+
+    def start_big(peer):
+        by_core(lambda c: big(peer, lat, c).start())
+
+    middle = has_up & has_down
+
+    def send_far():
+        last = n_lat - 2
+        each(last, lambda j: pl.when(far_off(peer_of(last - j)))(lambda: start_small(peer_of(last - j))))
+        each(n_lat - 1, lambda j: start_big(peer_of(last - j)))
+
+    def far_off(peer):
+        return (peer > lat + 1) | (peer < lat - 1)
+
+    def send_near_small():
+        pl.when(has_up)(lambda: start_small(lat - 1))
+        pl.when(has_down)(lambda: start_small(lat + 1))
 
     def put_row(taps, r, v):
         taps[r * pitch : (r + 1) * pitch, 0:chans] = pltpu.roll(v, 1, 0).astype(BF16)
@@ -240,10 +301,8 @@
     def conv(taps, kind, first, count):
         acc = None
         for a in range(3):
-            part = jnp.dot(
-                taps[(first + a) * pitch : (first + a + count) * pitch, :], kw[kind, a],
-                preferred_element_type=F32,
-            )
+            parts = [taps[(f + a) * pitch : (f + a + count) * pitch, :] for f in first]
+            part = jnp.dot(jnp.concatenate(parts, axis=0), kw[kind, a], preferred_element_type=F32)
             acc = part if acc is None else acc + part
         return acc
 
@@ -275,7 +334,7 @@
     def x_routes():
         i = 0
         routes = {-1: [], 0: [], 1: []}
-        for dl, side in [(0, -1), (0, 1), (-1, 0), (-1, -1), (-1, 1), (1, 0), (1, -1), (1, 1)]:
+        for dl, side in [(-1, -1), (-1, 1), (1, -1), (1, 1)]:
             sr, dr, nr = span_r[dl]
             sc, dc, nc = span_c[side]
             routes[dl].append(remote(X, at(dl, side), sr, dr, nr, sc, dc, nc, i))
@@ -335,38 +394,43 @@
             jnp.concatenate([both[0, r], both[1, r]], axis=0).astype(F32).T.astype(BF16)
         )
     x_halo = x_routes()
-    halo_start(x_halo, (-1, 1, 0))
-
-    @pl.when(lat >= 2)
+    halo_start(x_halo, (-1, 1))
+
+    send_near_small()
+
+    @pl.when(middle)
     def _():
-        pl.semaphore_wait(heard_up, 1)
-
-        @pl.when(has_down)
-        def _():
+        @pl.when(lat >= 2)
+        def _():
+            pl.semaphore_wait(heard_up, 1)
             tell(heard_up, 1)
 
-    @pl.when(lat <= n_lat - 3)
-    def _():
-        pl.semaphore_wait(heard_down, 1)
-
-        @pl.when(has_up)
-        def _():
+        @pl.when(lat <= n_lat - 3)
+        def _():
+            pl.semaphore_wait(heard_down, 1)
             tell(heard_down, -1)
 
-    each(n_lat - 1, lambda j: start_pay(j, False, slice(0, 2)))
-    each(n_lat - 1, lambda j: start_pay(j, False, slice(2, 3)))
+        send_far()
 
     R[lat, ch] = pay[lat]
     R_at[lat] = pay_at[lat]
     R_p[lat] = pay_p[lat]
 
-    def forward(t):
-        return pltpu.make_async_remote_copy(
-            src_ref=R.at[t, ch], dst_ref=R.at[t, ch], send_sem=fwd_s.at[t], recv_sem=fwd_r.at[t],
+    def forward(t, c):
+        part = pl.ds(0, half * (1 + c))
+        return pltpu.make_async_remote_copy(
+            src_ref=R.at[t, c, :, part], dst_ref=R.at[t, c, :, part], send_sem=fwd_s.at[t], recv_sem=fwd_r.at[t],
             device_id=sibling, device_id_type=MESH,
         )
 
-    forward(lat).start()
+    def forward_small(t, kind):
+        ref, ss, rs = ((R_at, fat_s, fat_r), (R_p, fp_s, fp_r))[kind]
+        return pltpu.make_async_remote_copy(
+            src_ref=ref.at[t], dst_ref=ref.at[t], send_sem=ss.at[t], recv_sem=rs.at[t],
+            device_id=sibling, device_id_type=MESH,
+        )
+
+    by_core(lambda c: forward(lat, c).start())
     for load in loads[4:]:
         load.wait()
     for kind, k in enumerate((kin, kout, kout, kin)):
@@ -376,57 +440,101 @@
                 kw[kind, a, b * chans : (b + 1) * chans] = tap
     Z[...] = jnp.zeros(Z.shape, F32)
 
-    def hidden_rows(r0, count):
-        acc = conv(X3, 0, r0, count) + bias[...]
+    @pl.when(jnp.logical_not(middle))
+    def _():
+        @pl.when(lat >= 2)
+        def _():
+            pl.semaphore_wait(heard_up, 1)
+
+        @pl.when(lat <= n_lat - 3)
+        def _():
+            pl.semaphore_wait(heard_down, 1)
+
+        send_far()
+
+    def hidden_rows(first, count):
+        acc = conv(X3, 0, first, count) + bias[...]
         s = sigmoid(acc)
-        slope[r0 * pitch : (r0 + count) * pitch, :] = s * (1.0 + acc * (1.0 - s))
+        steep = s * (1.0 + acc * (1.0 - s))
         h = acc * s
-        for i in range(count):
-            row = h[i * pitch : (i + 1) * pitch]
-            f = edge_factor(r0 + i)
+        for i, r in enumerate(f + n for f in first for n in range(count)):
+            own = slice(i * pitch, (i + 1) * pitch)
+            slope[r * pitch : (r + 1) * pitch, :] = steep[own]
+            row = h[own]
+            f = edge_factor(r)
             if f is not None:
                 row = row * f
-            put_row(H3, r0 + i, row.astype(BF16).astype(F32))
-
-    halo_finish(x_halo, (0,))
+            put_row(H3, r, row.astype(BF16).astype(F32))
+
+    for copy in edges:
+        copy.wait_send()
+    edge_got(other, other).wait_recv()
+    for c in (0, 1):
+        edge_got(ch, c).wait_recv()
+    for side in (0, 1):
+        turned = jnp.concatenate([edge_r[side, 0], edge_r[side, 1]], axis=0).astype(F32).T.astype(BF16)
+        for r in range(rows):
+            X[top + r, side * (left + width) : side * (left + width) + SIDE] = turned[r * SIDE : (r + 1) * SIDE]
     for r in range(top, top + rows):
         put_row(X3, r, X[r].astype(F32))
     for r0 in range(HALO, rows, 2):
-        hidden_rows(r0, 2)
+        hidden_rows([r0], 2)
     swaps = []
 
-    def denoise_rows(r0, count):
-        acc = conv(H3, 1, r0, count)
-        for i in range(count):
-            r = r0 + i
+    def denoise_rows(first, count):
+        acc = conv(H3, 1, first, count)
+        for i, r in enumerate(f + n for f in first for n in range(count)):
             state = X[top + r, left : left + width].astype(F32)
             den = (state + acc[i * pitch + left : i * pitch + left + width]).astype(BF16)
             den_s[r] = den
             wide = den.astype(F32)
             base[r * width : (r + 1) * width, :] = keep_rate * state + blend_rate * wide
             DF[pl.ds(pl.multiple_of(r * cols + ch * width, width), width), :] = wide
-        part = pl.ds(r0, count)
-        swaps.append((r0, count, pair_copy(den_s.at[part], den_r.at[part], 1 + len(swaps))))
-        swaps[-1][2].start()
-
-    inner = [(r0, min(WIDE, rows - HALO - r0)) for r0 in range(HALO, rows - HALO, WIDE)]
-    outer = [(0, HALO), (rows - HALO, HALO)]
-    for r0, count in inner:
-        denoise_rows(r0, count)
+        for f in first:
+            part = pl.ds(f, count)
+            swaps.append((f, count, pair_copy(den_s.at[part], den_r.at[part], 1 + len(swaps))))
+            swaps[-1][2].start()
+
+    inner = [([r0], min(WIDE, rows - HALO - r0)) for r0 in range(HALO, rows - HALO, WIDE)]
+    outer = [([0, rows - HALO], HALO)]
+    for first, count in inner:
+        denoise_rows(first, count)
     halo_finish(x_halo, (-1, 1))
+    for dl in (-1, 1):
+        @pl.when(has_up if dl < 0 else has_down)
+        def _(dl=dl):
+            for mine in (0, 1):
+                raw_row(dl, mine).wait_send()
+            for c in (0, 1):
+                raw_got(dl, c).wait_recv()
+            for i in range(HALO):
+                side = 0 if dl < 0 else 1
+                X[side * (top + rows) + i, left : left + width] = (
+                    jnp.concatenate([raw[side, 0, i], raw[side, 1, i]], axis=0).astype(F32).T.astype(BF16)
+                )
+
     for r in (0, 1, top + rows, top + rows + 1):
         put_row(X3, r, X[r].astype(F32))
-    hidden_rows(0, HALO)
-    hidden_rows(rows, HALO)
-    for r0, count in outer:
-        denoise_rows(r0, count)
+    hidden_rows([0, rows], HALO)
+    for first, count in outer:
+        denoise_rows(first, count)
 
     def local_copy(t):
         return pltpu.make_async_copy(R_at.at[t], at_s.at[t], copy_sem.at[t])
 
     def take_at(j):
         peer = peer_of(j)
-        arrival(0, peer).wait()
+
+        @pl.when(ch == 1)
+        def _():
+            for kind in (0, 1):
+                small(peer, peer, kind).wait()
+                forward_small(peer, kind).start()
+
+        @pl.when(ch == 0)
+        def _():
+            forward_small(peer, 0).wait_recv()
+
         local_copy(peer).start()
 
     local_copy(lat).start()
@@ -434,11 +542,23 @@
 
     def take_pay(j):
         peer = peer_of(j)
-        for kind in (1, 2):
-            arrival(kind, peer).wait()
-        forward(peer).start()
-
-    each(n_lat - 1, take_pay)
+
+        def go(c):
+            big(peer, peer, c).wait()
+            forward(peer, c).start()
+
+        by_core(go)
+
+    def take_from(j0):
+        each(n_lat - 1 - j0, lambda j: take_pay(j + j0))
+
+    batches = slots // GROUP
+    split = batches == 2
+    if split:
+        take_pay(0)
+        pl.when(middle)(lambda: take_from(1))
+    else:
+        take_from(0)
     for r0, count, swap in swaps:
         swap.wait()
         for r in range(r0, r0 + count):
@@ -475,24 +595,42 @@
     def source_of(j):
         return jnp.where(j == 0, lat, peer_of(jnp.maximum(j - 1, 0)))
 
-    def observe(g, first):
+    def settle(t):
+        def go(c):
+            forward(t, c).wait_send()
+            forward(t, 1 - c).wait_recv()
+
+        by_core(go)
+
+        @pl.when((ch == 0) & (t != lat))
+        def _():
+            forward_small(t, 1).wait_recv()
+
+        @pl.when((ch == 1) & (t != lat))
+        def _():
+            for kind in (0, 1):
+                forward_small(t, kind).wait_send()
+
+    g_halo = g_routes()
+
+    def observe(g, first, last):
         owners = [source_of(g * sources + i) for i in range(sources)]
         for t in owners:
-            forward(t).wait()
+            settle(t)
         for i in range(GROUP):
             t, k = owners[i // CAP], i % CAP
             row, lane = corner()
-            tri = jnp.concatenate([R[t, 0, k, 0:quarter], R[t, 1, k, 0:quarter]], axis=0).astype(F32)
+            tri = R[t, 1, k, half:chans].astype(F32)
             upper = jnp.where((lane <= row) | (lane >= half), tri, 0.0)
             lower = jnp.where(lane > row + half, pltpu.roll(tri, half, 1), 0.0)
             lower = jnp.where(lane == row + half, R_p[t, k : k + 1, :], lower)
             side = jnp.concatenate([upper, lower], axis=0).astype(BF16)
             normal = side + side.T
-            pull = jnp.concatenate([R[t, 0, k, quarter:packed], R[t, 1, k, quarter:packed]], axis=0)
+            pull = jnp.concatenate([R[t, 0, k, 0:half], R[t, 1, k, 0:half]], axis=0)
             pulled = jnp.dot(normal, patches[t, k], preferred_element_type=F32) - pull.astype(F32).T
             for a in range(PH):
                 Z[pl.ds((i * PH + a) * strip + reach, PW), :] = pulled[a * PW : (a + 1) * PW]
-        for r in (0, 1, rows - 2, rows - 1, *range(2, rows - 2)):
+        for n, r in enumerate((0, 1, rows - 2, rows - 1, *range(2, rows - 2))):
             total = None
             for i in range(GROUP):
                 t, k = owners[i // CAP], i % CAP
@@ -506,44 +644,54 @@
             if not first:
                 total = total + GW[span_w, :]
             GW[span_w, :] = total
-            G[top + r, pl.ds(pl.multiple_of(other * SIDE, SIDE), reach)] = total.astype(BF16)
-
-    observe(0, True)
-    if slots != GROUP:
-        lax.fori_loop(1, slots // GROUP, lambda g, _: observe(g, False) or 0, 0)
-    g_halo = g_routes()
-    halo_start(g_halo, (-1, 1, 0))
-
-    def grad_rows(r0, count):
-        g = conv(X3, 2, r0, count) * slope[r0 * pitch : (r0 + count) * pitch, :]
-        for i in range(count):
-            row = g[i * pitch : (i + 1) * pitch]
-            f = edge_factor(r0 + i)
+            if last:
+                G[top + r, pl.ds(pl.multiple_of(other * SIDE, SIDE), reach)] = total.astype(BF16)
+                if n == 3:
+                    halo_start(g_halo, (-1, 1))
+        if last:
+            halo_start(g_halo, (0,))
+
+    if split:
+        observe(0, True, False)
+        pl.when(jnp.logical_not(middle))(lambda: take_from(1))
+        observe(1, False, True)
+    elif batches == 1:
+        observe(0, True, True)
+    else:
+        observe(0, True, False)
+        lax.fori_loop(1, batches - 1, lambda g, _: observe(g, False, False) or 0, 0)
+        observe(batches - 1, False, True)
+
+    def grad_rows(first, count):
+        back = conv(X3, 2, first, count)
+        for i, r in enumerate(f + n for f in first for n in range(count)):
+            row = back[i * pitch : (i + 1) * pitch] * slope[r * pitch : (r + 1) * pitch, :]
+            f = edge_factor(r)
             if f is not None:
                 row = row * f
-            put_row(H3, r0 + i, row.astype(BF16).astype(F32))
+            put_row(H3, r, row.astype(BF16).astype(F32))
 
     halo_finish(g_halo, (0,))
     for r in range(top, top + rows):
         put_row(X3, r, G[r].astype(F32))
     for r0 in range(HALO, rows, 2):
-        grad_rows(r0, 2)
+        grad_rows([r0], 2)
     back_home = []
 
-    def finish_rows(r0, count):
-        acc = conv(H3, 3, r0, count)
-        for i in range(count):
-            r = r0 + i
+    def finish_rows(first, count):
+        acc = conv(H3, 3, first, count)
+        for i, r in enumerate(f + n for f in first for n in range(count)):
             grad = GW[r * pitch + left : r * pitch + left + width, :] + acc[i * pitch + left : i * pitch + left + width]
             res = (base[r * width : (r + 1) * width, :] - guide_rate * grad).T
             out_s[r] = jnp.where(ch == 0, res[half:chans], res[0:half]).astype(BF16)
             out_h[0, pl.ds(r, half, stride=rows), :] = jnp.where(ch == 0, res[0:half], res[half:chans])
-        part = pl.ds(r0, count)
-        back_home.append((r0, count, pair_copy(out_s.at[part], out_r.at[part], 1 + len(swaps) + len(back_home))))
-        back_home[-1][2].start()
-
-    for r0, count in inner:
-        finish_rows(r0, count)
+        for f in first:
+            part = pl.ds(f, count)
+            back_home.append((f, count, pair_copy(out_s.at[part], out_r.at[part], 1 + len(swaps) + len(back_home))))
+            back_home[-1][2].start()
+
+    for first, count in inner:
+        finish_rows(first, count)
     each(n_lat - 1, lambda j: patch_copy(peer_of(j), peer_of(j)).wait())
 
     def innovate(b):
@@ -557,10 +705,9 @@
     halo_finish(g_halo, (-1, 1))
     for r in (0, 1, top + rows, top + rows + 1):
         put_row(X3, r, G[r].astype(F32))
-    grad_rows(0, HALO)
-    grad_rows(rows, HALO)
-    for r0, count in outer:
-        finish_rows(r0, count)
+    grad_rows([0, rows], HALO)
+    for first, count in outer:
+        finish_rows(first, count)
     mine = pl.ds(pl.multiple_of(ch * width, width), width)
     theirs = pl.ds(pl.multiple_of(other * width, width), width)
     out[:, mine] = out_h[0]
@@ -619,6 +766,11 @@
             pltpu.VMEM((4, 3, 3 * chans, chans), BF16),
             dma((6,)),
             pltpu.VMEM((2, rows, half, width), BF16),
+            pltpu.VMEM((4, half, width), BF16),
+            pltpu.VMEM((2, 2, half, width), BF16),
+            pltpu.VMEM((2, 2, HALO, half, width), BF16),
+            dma((3,)), dma((4,)),
+            dma((4,)), dma((4,)),
             pltpu.VMEM((rows + 4, pitch, chans), BF16),
             pltpu.VMEM(((rows + 4) * pitch, 3 * chans), BF16),
             pltpu.VMEM(((rows + 2) * pitch, 3 * chans), BF16),
@@ -627,13 +779,13 @@
             pltpu.VMEM((rows * cols, chans), F32),
             pltpu.VMEM((rows, width, chans), BF16),
             pltpu.VMEM((rows, width, chans), BF16),
-            pltpu.VMEM((blocks, half // 2, cells), F32),
+            pltpu.VMEM((blocks, half, cells), F32),
             pltpu.VMEM((blocks, half, cells), F32),
             pltpu.VMEM((blocks, cells), F32),
-            pltpu.VMEM((n_lat, CAP, half + half // 2, cells), BF16),
+            pltpu.VMEM((n_lat, CAP, chans, cells), BF16),
             pltpu.VMEM((n_lat, SMALL, obs), I32),
             pltpu.VMEM((n_lat, SMALL, obs), F32),
-            pltpu.VMEM((n_lat, 2, CAP, half + half // 2, cells), BF16),
+            pltpu.VMEM((n_lat, 2, CAP, chans, cells), BF16),
             pltpu.VMEM((n_lat, SMALL, obs), I32),
             pltpu.VMEM((n_lat, SMALL, obs), F32),
             pltpu.SMEM((n_lat, SMALL, obs), I32),
@@ -655,11 +807,13 @@
             dma((n_lat,)), dma((n_lat,)),
             dma((n_lat,)), dma((n_lat,)),
             dma((n_lat,)), dma((n_lat,)),
+            dma((n_lat,)), dma((n_lat,)),
+            dma((n_lat,)), dma((n_lat,)),
             dma((n_lat,)),
             dma((n_lat,)), dma((n_lat,)),
         ],
         compiler_params=pltpu.CompilerParams(
-            collective_id=0, has_side_effects=True, vmem_limit_bytes=(63 if slots <= GROUP else 48) * 1024 * 1024
+            collective_id=0, has_side_effects=True, vmem_limit_bytes=(63 if slots <= 2 * GROUP else 48) * 1024 * 1024
         ),
     )
     out, innovation = call(

time: 25.9 us -> 24.7 us (0.954)
  Pallas kernels: 25.1 us -> 23.9 us
    pallas_call x1, Pallas kernels: 24.3 us -> 23.1 us  [body(): call(dest_tile, row_offset, col_offset, noisy_state, kernel_in, kernel_ou...]
where the time goes in v4:
time: 24.7 us; the launch traced here: 24.5 us
  Pallas kernels  23.9 us (97%)
  between operations  0.64 us (3%)
    pallas_call x1, Pallas kernels, body(): call(dest_tile, row_offset, col_offset, noisy_state, kernel_in, kernel_ou...  23.1 us
    pallas_call x1, Pallas kernels, body(): pl.pallas_call(store, out_shape=(jax.ShapeDtypeStruct((half * rows, cols)...  0.82 us

profile of v4, /device:TPU:0, one launch (start us, length us, event | category | flops | bytes accessed | tf_op | source)
XLA Modules:
  0.0 24.5 jit_solution(9022997228115442849)
XLA Ops:
  0.6 23.1 %shard_map.113 = (f32[512,256]{1,0:T(8,128)S(1)}, bf16[4,64,128]{2,1,0:T(8,128)(2,1)S(1)}) custom-call(s32[4]{0:T(128)} %dest.1, s32[4]{0:T(128)} %row_off.1, s32[4]{0:T(128)} %col_off.1, bf16[64,8,256]{2,1,0:T(8,128)(2,1)} %x_hbm.1, bf16[3,3,128,128]{3,2,1,0:T(8,128)(2,1)} %kin_hbm.1, bf16[3,3,128,128]{3,2,1,0:T(8,128)(2,1)} %kout_hbm.1, f32[1,128]{1,0:T(1,128)} %bitcast.2, ...), custom_call_target="tpu_custom_call" | custom-call | tf_op jit(solution)/shard_map/pallas_call | solution.py:819
  23.7 0.8 %shard_map.114 = (f32[512,256]{1,0:T(8,128)}, bf16[4,64,128]{2,1,0:T(8,128)(2,1)}) custom-call(f32[512,256]{1,0:T(8,128)S(1)} %get-tuple-element.6.out, bf16[4,64,128]{2,1,0:T(8,128)(2,1)S(1)} %get-tuple-element.7.innovation), custom_call_target="tpu_custom_call" | custom-call | tf_op jit(solution)/shard_map/pallas_call | solution.py:823

commit v5 on v4

--- a/solution.py
+++ b/solution.py
@@ -40,13 +40,14 @@
 
 def kernel(
     n_lat, n_lon, rows, width, half, blocks,
-    dest, row_off, col_off, x_hbm, kin_hbm, kout_hbm, bias, weight_hbm, values_hbm, scale_hbm,
+    dest_hbm, row_hbm, col_hbm, x_hbm, kin_hbm, kout_hbm, bias_hbm, weight_hbm, values_hbm, scale_hbm,
     out, inn_out,
+    dest, row_off, col_off, bias,
     xv, xs, x_send, kin, kout, weight, values, scale_raw, scale, kw, load_sem,
     both, edge, edge_r, raw, edge_ss, edge_rs, raw_s, raw_r, X, X3, H3, slope, base, DF, den_s, den_r, block_a, block_b, block_d,
-    pay, pay_at, pay_p, R, R_at, R_p, at_s, patches, pat_s, pat_r, Z, G, GW, out_h, out_s, out_r,
+    pay, pay_at, pay_p, R, R_p, at_s, patches, pat_s, pat_r, Z, G, GW, out_h, out_s, out_r,
     plan, heard_up, heard_down,
-    halo_s, halo_r, pair_s, pair_r, pay_ss, pay_rs, at_ss, at_rs, p_ss, p_rs, fwd_s, fwd_r, fat_s, fat_r, fp_s, fp_r, copy_sem, pat_ss, pat_rs,
+    halo_s, halo_r, pair_s, pair_r, pay_ss, pay_rs, at_ss, at_rs, p_ss, p_rs, fwd_s, fwd_r, fp_s, copy_sem, pat_ss, pat_rs,
 ):
     lat, lon, ch = lax.axis_index("lat"), lax.axis_index("lon"), lax.axis_index("ch")
     other = 1 - ch
@@ -87,8 +88,9 @@
     loads = [
         pltpu.make_async_copy(src, dst, load_sem.at[i])
         for i, (src, dst) in enumerate(
-            [(x_hbm, xv), (weight_hbm, weight), (values_hbm, values), (scale_hbm, scale_raw),
-             (kin_hbm, kin), (kout_hbm, kout)]
+            [(x_hbm, xv), (dest_hbm, dest), (row_hbm, row_off), (col_hbm, col_off),
+             (weight_hbm, weight), (values_hbm, values), (scale_hbm, scale_raw),
+             (kin_hbm, kin), (kout_hbm, kout), (bias_hbm, bias)]
         )
     ]
     for load in loads:
@@ -114,21 +116,6 @@
     def _():
         for side in (-1, 0, 1):
             greet(at(1, side))
-
-    def count_block(b, _):
-        def earlier(e, rank):
-            return rank + jnp.where(dest[e] == dest[b], 1, 0)
-
-        plan[b] = dest[b] * CAP + lax.fori_loop(0, b, earlier, 0)
-        return 0
-
-    for b in range(blocks) if blocks <= 8 else ():
-        rank = 0
-        for e in range(b):
-            rank = rank + jnp.where(dest[e] == dest[b], 1, 0)
-        plan[b] = dest[b] * CAP + rank
-    if blocks > 8:
-        lax.fori_loop(0, blocks, count_block, 0)
 
     def corner():
         return (
@@ -207,7 +194,7 @@
         src = both.at[ch, pl.ds(row, HALO)] if mine else x_send.at[pl.ds(row, HALO)]
         side = 1 if dl < 0 else 0
         return pltpu.make_async_remote_copy(
-            src_ref=src, dst_ref=raw.at[side, ch], send_sem=raw_s.at[2 * side + mine],
+            src_ref=src, dst_ref=raw.at[side, ch], send_sem=raw_s.at[side],
             recv_sem=raw_r.at[2 * side + ch],
             device_id={"lat": lat + dl, "ch": ch if mine else other}, device_id_type=MESH,
         )
@@ -215,19 +202,19 @@
     def raw_got(dl, c):
         side = 0 if dl < 0 else 1
         return pltpu.make_async_remote_copy(
-            src_ref=x_send.at[pl.ds(0, HALO)], dst_ref=raw.at[side, c], send_sem=raw_s.at[2 * side],
+            src_ref=x_send.at[pl.ds(0, HALO)], dst_ref=raw.at[side, c], send_sem=raw_s.at[side],
             recv_sem=raw_r.at[2 * side + c], device_id={"lat": lat + dl}, device_id_type=MESH,
         )
 
     def edge_copy(n, src, side, place):
         return pltpu.make_async_remote_copy(
-            src_ref=edge.at[src], dst_ref=edge_r.at[side, ch], send_sem=edge_ss.at[n],
+            src_ref=edge.at[src], dst_ref=edge_r.at[side, ch], send_sem=edge_ss,
             recv_sem=edge_rs.at[2 * side + ch], device_id=place, device_id_type=MESH,
         )
 
     def edge_got(side, c):
         return pltpu.make_async_remote_copy(
-            src_ref=edge.at[0], dst_ref=edge_r.at[side, c], send_sem=edge_ss.at[0],
+            src_ref=edge.at[0], dst_ref=edge_r.at[side, c], send_sem=edge_ss,
             recv_sem=edge_rs.at[2 * side + c], device_id=sibling, device_id_type=MESH,
         )
 
@@ -244,8 +231,23 @@
     ]
     for copy in edges:
         copy.start()
-    for load in loads[1:4]:
+    for load in loads[1:7]:
         load.wait()
+    def count_block(b, _):
+        def earlier(e, rank):
+            return rank + jnp.where(dest[e] == dest[b], 1, 0)
+
+        plan[b] = dest[b] * CAP + lax.fori_loop(0, b, earlier, 0)
+        return 0
+
+    for b in range(blocks) if blocks <= 8 else ():
+        rank = 0
+        for e in range(b):
+            rank = rank + jnp.where(dest[e] == dest[b], 1, 0)
+        plan[b] = dest[b] * CAP + rank
+    if blocks > 8:
+        lax.fori_loop(0, blocks, count_block, 0)
+
     scale[...] = scale_raw[...].astype(F32)
     pay_at[...] = jnp.zeros(pay_at.shape, I32)
     pay_p[...] = jnp.zeros(pay_p.shape, F32)
@@ -259,21 +261,22 @@
         part = pl.ds(0, half * (1 + c))
         return pltpu.make_async_remote_copy(
             src_ref=pay.at[peer, :, part], dst_ref=R.at[landing, c, :, part],
-            send_sem=pay_ss.at[peer], recv_sem=pay_rs.at[landing],
+            send_sem=pay_ss, recv_sem=pay_rs.at[landing],
             device_id={"lat": peer}, device_id_type=MESH,
         )
 
     def small(peer, landing, kind):
-        src, dst, ss, rs = ((pay_at, R_at, at_ss, at_rs), (pay_p, R_p, p_ss, p_rs))[kind]
-        return pltpu.make_async_remote_copy(
-            src_ref=src.at[peer], dst_ref=dst.at[landing], send_sem=ss.at[peer], recv_sem=rs.at[landing],
+        src, dst, ss, rs = ((pay_at, at_s, at_ss, at_rs), (pay_p, R_p, p_ss, p_rs))[kind]
+        return pltpu.make_async_remote_copy(
+            src_ref=src.at[peer], dst_ref=dst.at[landing], send_sem=ss, recv_sem=rs.at[landing],
             device_id={"lat": peer}, device_id_type=MESH,
         )
 
     def start_small(peer):
+        small(peer, lat, 0).start()
+
         @pl.when(ch == 1)
         def _():
-            small(peer, lat, 0).start()
             small(peer, lat, 1).start()
 
     def start_big(peer):
@@ -281,10 +284,12 @@
 
     middle = has_up & has_down
 
+    def upward(j):
+        return j + jnp.where(lat <= j, 1, 0)
+
     def send_far():
-        last = n_lat - 2
-        each(last, lambda j: pl.when(far_off(peer_of(last - j)))(lambda: start_small(peer_of(last - j))))
-        each(n_lat - 1, lambda j: start_big(peer_of(last - j)))
+        each(n_lat - 1, lambda j: pl.when(far_off(upward(j)))(lambda: start_small(upward(j))))
+        each(n_lat - 1, lambda j: start_big(upward(j)))
 
     def far_off(peer):
         return (peer > lat + 1) | (peer < lat - 1)
@@ -342,7 +347,7 @@
         return routes
 
     def g_routes():
-        i = 8
+        i = 4
         routes = {-1: [], 0: [], 1: []}
         out_src = left + ch * (width - SIDE)
         out_dst = other * (left + width)
@@ -413,25 +418,25 @@
         send_far()
 
     R[lat, ch] = pay[lat]
-    R_at[lat] = pay_at[lat]
+    own_at = pltpu.make_async_copy(pay_at.at[lat], at_s.at[lat], copy_sem)
+    own_at.start()
     R_p[lat] = pay_p[lat]
 
     def forward(t, c):
         part = pl.ds(0, half * (1 + c))
         return pltpu.make_async_remote_copy(
-            src_ref=R.at[t, c, :, part], dst_ref=R.at[t, c, :, part], send_sem=fwd_s.at[t], recv_sem=fwd_r.at[t],
+            src_ref=R.at[t, c, :, part], dst_ref=R.at[t, c, :, part], send_sem=fwd_s, recv_sem=fwd_r.at[t],
             device_id=sibling, device_id_type=MESH,
         )
 
-    def forward_small(t, kind):
-        ref, ss, rs = ((R_at, fat_s, fat_r), (R_p, fp_s, fp_r))[kind]
-        return pltpu.make_async_remote_copy(
-            src_ref=ref.at[t], dst_ref=ref.at[t], send_sem=ss.at[t], recv_sem=rs.at[t],
+    def forward_small(t):
+        return pltpu.make_async_remote_copy(
+            src_ref=R_p.at[t], dst_ref=R_p.at[t], send_sem=fp_s, recv_sem=p_rs.at[t],
             device_id=sibling, device_id_type=MESH,
         )
 
     by_core(lambda c: forward(lat, c).start())
-    for load in loads[4:]:
+    for load in loads[7:]:
         load.wait()
     for kind, k in enumerate((kin, kout, kout, kin)):
         for a in range(3):
@@ -466,8 +471,10 @@
                 row = row * f
             put_row(H3, r, row.astype(BF16).astype(F32))
 
-    for copy in edges:
-        copy.wait_send()
+    pltpu.make_async_remote_copy(
+        src_ref=edge.at[0:3], dst_ref=edge.at[0:3], send_sem=edge_ss, recv_sem=edge_rs.at[0],
+        device_id=sibling, device_id_type=MESH,
+    ).wait_send()
     edge_got(other, other).wait_recv()
     for c in (0, 1):
         edge_got(ch, c).wait_recv()
@@ -503,8 +510,11 @@
     for dl in (-1, 1):
         @pl.when(has_up if dl < 0 else has_down)
         def _(dl=dl):
-            for mine in (0, 1):
-                raw_row(dl, mine).wait_send()
+            pltpu.make_async_remote_copy(
+                src_ref=x_send.at[pl.ds(0, 2 * HALO)], dst_ref=x_send.at[pl.ds(0, 2 * HALO)],
+                send_sem=raw_s.at[1 if dl < 0 else 0], recv_sem=raw_r.at[0],
+                device_id=sibling, device_id_type=MESH,
+            ).wait_send()
             for c in (0, 1):
                 raw_got(dl, c).wait_recv()
             for i in range(HALO):
@@ -519,33 +529,18 @@
     for first, count in outer:
         denoise_rows(first, count)
 
-    def local_copy(t):
-        return pltpu.make_async_copy(R_at.at[t], at_s.at[t], copy_sem.at[t])
-
-    def take_at(j):
-        peer = peer_of(j)
-
-        @pl.when(ch == 1)
-        def _():
-            for kind in (0, 1):
-                small(peer, peer, kind).wait()
-                forward_small(peer, kind).start()
-
-        @pl.when(ch == 0)
-        def _():
-            forward_small(peer, 0).wait_recv()
-
-        local_copy(peer).start()
-
-    local_copy(lat).start()
-    each(n_lat - 1, take_at)
+    own_at.wait()
+    each(n_lat - 1, lambda j: small(peer_of(j), peer_of(j), 0).wait_recv())
 
     def take_pay(j):
         peer = peer_of(j)
 
         def go(c):
-            big(peer, peer, c).wait()
+            big(peer, peer, c).wait_recv()
             forward(peer, c).start()
+            if c == 1:
+                small(peer, peer, 1).wait_recv()
+                forward_small(peer).start()
 
         by_core(go)
 
@@ -555,15 +550,11 @@
     batches = slots // GROUP
     split = batches == 2
     if split:
-        take_pay(0)
-        pl.when(middle)(lambda: take_from(1))
-    else:
-        take_from(0)
+        pl.when(jnp.logical_not(middle))(lambda: take_pay(0))
     for r0, count, swap in swaps:
         swap.wait()
         for r in range(r0, r0 + count):
             DF[pl.ds(pl.multiple_of(r * cols + other * width, width), width), :] = den_r[r].astype(F32)
-    each(n_lat, lambda t: local_copy(t).wait())
 
     def gather(t):
         lane = lax.broadcasted_iota(I32, (half, chans), 1)
@@ -584,7 +575,7 @@
     def patch_copy(peer, landing):
         return pltpu.make_async_remote_copy(
             src_ref=pat_s.at[peer], dst_ref=pat_r.at[landing],
-            send_sem=pat_ss.at[peer], recv_sem=pat_rs.at[landing],
+            send_sem=pat_ss, recv_sem=pat_rs.at[landing],
             device_id={"lat": peer}, device_id_type=MESH,
         )
 
@@ -596,20 +587,32 @@
         return jnp.where(j == 0, lat, peer_of(jnp.maximum(j - 1, 0)))
 
     def settle(t):
-        def go(c):
-            forward(t, c).wait_send()
-            forward(t, 1 - c).wait_recv()
-
-        by_core(go)
+        by_core(lambda c: forward(t, 1 - c).wait_recv())
 
         @pl.when((ch == 0) & (t != lat))
         def _():
-            forward_small(t, 1).wait_recv()
-
-        @pl.when((ch == 1) & (t != lat))
-        def _():
-            for kind in (0, 1):
-                forward_small(t, kind).wait_send()
+            forward_small(t).wait_recv()
+
+    def drain(src, dst, sem):
+        pltpu.make_async_remote_copy(
+            src_ref=src, dst_ref=dst, send_sem=sem, recv_sem=pay_rs.at[0],
+            device_id=sibling, device_id_type=MESH,
+        ).wait_send()
+
+    def drain_all():
+        others = pl.ds(0, n_lat - 1)
+
+        def go(c):
+            part = pl.ds(0, half * (1 + c))
+            drain(pay.at[others, :, part], R.at[others, c, :, part], pay_ss)
+            drain(R.at[:, c, :, part], R.at[:, c, :, part], fwd_s)
+            if c == 1:
+                drain(pay_p.at[others], R_p.at[others], p_ss)
+                drain(R_p.at[others], R_p.at[others], fp_s)
+
+        by_core(go)
+        drain(pay_at.at[others], at_s.at[others], at_ss)
+        drain(pat_s.at[others], pat_r.at[others], pat_ss)
 
     g_halo = g_routes()
 
@@ -652,6 +655,10 @@
             halo_start(g_halo, (0,))
 
     if split:
+        pl.when(middle)(lambda: take_from(0))
+    else:
+        take_from(0)
+    if split:
         observe(0, True, False)
         pl.when(jnp.logical_not(middle))(lambda: take_from(1))
         observe(1, False, True)
@@ -692,7 +699,8 @@
 
     for first, count in inner:
         finish_rows(first, count)
-    each(n_lat - 1, lambda j: patch_copy(peer_of(j), peer_of(j)).wait())
+    each(n_lat - 1, lambda j: patch_copy(peer_of(j), peer_of(j)).wait_recv())
+    drain_all()
 
     def innovate(b):
         slot = plan[b]
@@ -743,7 +751,6 @@
     pairs = 1 + 2 * (2 - (HALO + HALO - rows) // WIDE)
     vmem = pl.BlockSpec(memory_space=pltpu.VMEM)
     hbm = pl.BlockSpec(memory_space=pltpu.HBM)
-    smem = pl.BlockSpec(memory_space=pltpu.SMEM)
     dma = pltpu.SemaphoreType.DMA
     call = pl.pallas_call(
         functools.partial(kernel, n_lat, n_lon, rows, width, half, blocks),
@@ -751,9 +758,13 @@
             pltpu.VMEM((half * rows, cols), F32),
             pltpu.VMEM((blocks, half, obs), BF16),
         ),
-        in_specs=[smem] * 3 + [hbm] * 3 + [vmem] + [hbm] * 3,
+        in_specs=[hbm] * 10,
         out_specs=(vmem, vmem),
         scratch_shapes=[
+            pltpu.SMEM((blocks,), I32),
+            pltpu.SMEM((blocks,), I32),
+            pltpu.SMEM((blocks,), I32),
+            pltpu.VMEM((1, chans), F32),
             pltpu.VMEM((half, rows, cols), BF16),
             pltpu.VMEM((2, half * rows, width), F32),
             pltpu.VMEM((rows, half, width), BF16),
@@ -764,13 +775,13 @@
             pltpu.VMEM(obs_precision.shape, BF16),
             pltpu.VMEM(obs_precision.shape, F32),
             pltpu.VMEM((4, 3, 3 * chans, chans), BF16),
-            dma((6,)),
+            dma((10,)),
             pltpu.VMEM((2, rows, half, width), BF16),
             pltpu.VMEM((4, half, width), BF16),
             pltpu.VMEM((2, 2, half, width), BF16),
             pltpu.VMEM((2, 2, HALO, half, width), BF16),
-            dma((3,)), dma((4,)),
-            dma((4,)), dma((4,)),
+            dma, dma((4,)),
+            dma((2,)), dma((4,)),
             pltpu.VMEM((rows + 4, pitch, chans), BF16),
             pltpu.VMEM(((rows + 4) * pitch, 3 * chans), BF16),
             pltpu.VMEM(((rows + 2) * pitch, 3 * chans), BF16),
@@ -786,7 +797,6 @@
             pltpu.VMEM((n_lat, SMALL, obs), I32),
             pltpu.VMEM((n_lat, SMALL, obs), F32),
             pltpu.VMEM((n_lat, 2, CAP, chans, cells), BF16),
-            pltpu.VMEM((n_lat, SMALL, obs), I32),
             pltpu.VMEM((n_lat, SMALL, obs), F32),
             pltpu.SMEM((n_lat, SMALL, obs), I32),
             pltpu.VMEM((n_lat, CAP, cells, chans), BF16),
@@ -801,16 +811,15 @@
             pltpu.SMEM((blocks,), I32),
             pltpu.SemaphoreType.REGULAR,
             pltpu.SemaphoreType.REGULAR,
-            dma((13,)), dma((13,)),
+            dma((9,)), dma((9,)),
             dma((pairs,)), dma((pairs,)),
-            dma((n_lat,)), dma((n_lat,)),
-            dma((n_lat,)), dma((n_lat,)),
-            dma((n_lat,)), dma((n_lat,)),
-            dma((n_lat,)), dma((n_lat,)),
-            dma((n_lat,)), dma((n_lat,)),
-            dma((n_lat,)), dma((n_lat,)),
-            dma((n_lat,)),
-            dma((n_lat,)), dma((n_lat,)),
+            dma, dma((n_lat,)),
+            dma, dma((n_lat,)),
+            dma, dma((n_lat,)),
+            dma, dma((n_lat,)),
+            dma,
+            dma,
+            dma, dma((n_lat,)),
         ],
         compiler_params=pltpu.CompilerParams(
             collective_id=0, has_side_effects=True, vmem_limit_bytes=(63 if slots <= 2 * GROUP else 48) * 1024 * 1024

time: 24.7 us -> 23.4 us (0.947)
  Pallas kernels: 23.9 us -> 22.6 us
    pallas_call x1, Pallas kernels: 23.1 us -> 21.8 us  [body(): call(dest_tile, row_offset, col_offset, noisy_state, kernel_in, kernel_ou...]
where the time goes in v5:
time: 23.4 us; the launch traced here: 23.3 us
  Pallas kernels  22.6 us (97%)
  between operations  0.64 us (3%)
    pallas_call x1, Pallas kernels, body(): call(dest_tile, row_offset, col_offset, noisy_state, kernel_in, kernel_ou...  21.8 us
    pallas_call x1, Pallas kernels, body(): pl.pallas_call(store, out_shape=(jax.ShapeDtypeStruct((half * rows, cols)...  0.82 us

profile of v5, /device:TPU:0, one launch (start us, length us, event | category | flops | bytes accessed | tf_op | source)
XLA Modules:
  0.0 23.3 jit_solution(1875919635034596280)
XLA Ops:
  0.6 21.8 %shard_map.113 = (f32[512,256]{1,0:T(8,128)S(1)}, bf16[4,64,128]{2,1,0:T(8,128)(2,1)S(1)}) custom-call(s32[4]{0:T(128)} %dest_hbm.1, s32[4]{0:T(128)} %row_hbm.1, s32[4]{0:T(128)} %col_hbm.1, bf16[64,8,256]{2,1,0:T(8,128)(2,1)} %x_hbm.1, bf16[3,3,128,128]{3,2,1,0:T(8,128)(2,1)} %kin_hbm.1, bf16[3,3,128,128]{3,2,1,0:T(8,128)(2,1)} %kout_hbm.1, ...), custom_call_target="tpu_custom_call" | custom-call | tf_op jit(solution)/shard_map/pallas_call | solution.py:828
  22.5 0.8 %shard_map.114 = (f32[512,256]{1,0:T(8,128)}, bf16[4,64,128]{2,1,0:T(8,128)(2,1)}) custom-call(f32[512,256]{1,0:T(8,128)S(1)} %get-tuple-element.6.out, bf16[4,64,128]{2,1,0:T(8,128)(2,1)S(1)} %get-tuple-element.7.innovation), custom_call_target="tpu_custom_call" | custom-call | tf_op jit(solution)/shard_map/pallas_call | solution.py:832

commit v6 on v5

--- a/solution.py
+++ b/solution.py
@@ -195,27 +195,21 @@
         side = 1 if dl < 0 else 0
         return pltpu.make_async_remote_copy(
             src_ref=src, dst_ref=raw.at[side, ch], send_sem=raw_s.at[side],
-            recv_sem=raw_r.at[2 * side + ch],
+            recv_sem=raw_r.at[side],
             device_id={"lat": lat + dl, "ch": ch if mine else other}, device_id_type=MESH,
         )
 
-    def raw_got(dl, c):
-        side = 0 if dl < 0 else 1
-        return pltpu.make_async_remote_copy(
-            src_ref=x_send.at[pl.ds(0, HALO)], dst_ref=raw.at[side, c], send_sem=raw_s.at[side],
-            recv_sem=raw_r.at[2 * side + c], device_id={"lat": lat + dl}, device_id_type=MESH,
-        )
-
     def edge_copy(n, src, side, place):
         return pltpu.make_async_remote_copy(
             src_ref=edge.at[src], dst_ref=edge_r.at[side, ch], send_sem=edge_ss,
-            recv_sem=edge_rs.at[2 * side + ch], device_id=place, device_id_type=MESH,
-        )
-
-    def edge_got(side, c):
-        return pltpu.make_async_remote_copy(
-            src_ref=edge.at[0], dst_ref=edge_r.at[side, c], send_sem=edge_ss,
-            recv_sem=edge_rs.at[2 * side + c], device_id=sibling, device_id_type=MESH,
+            recv_sem=edge_rs.at[n // 2], device_id=place, device_id_type=MESH,
+        )
+
+    def edge_got(n, count):
+        part = pl.ds(0, count)
+        return pltpu.make_async_remote_copy(
+            src_ref=edge.at[part], dst_ref=edge.at[part], send_sem=edge_ss,
+            recv_sem=edge_rs.at[n], device_id=sibling, device_id_type=MESH,
         )
 
     for dl in (-1, 1):
@@ -266,9 +260,9 @@
         )
 
     def small(peer, landing, kind):
-        src, dst, ss, rs = ((pay_at, at_s, at_ss, at_rs), (pay_p, R_p, p_ss, p_rs))[kind]
-        return pltpu.make_async_remote_copy(
-            src_ref=src.at[peer], dst_ref=dst.at[landing], send_sem=ss, recv_sem=rs.at[landing],
+        src, dst, ss, rs = ((pay_at, at_s, at_ss, at_rs), (pay_p, R_p, p_ss, p_rs.at[landing]))[kind]
+        return pltpu.make_async_remote_copy(
+            src_ref=src.at[peer], dst_ref=dst.at[landing], send_sem=ss, recv_sem=rs,
             device_id={"lat": peer}, device_id_type=MESH,
         )
 
@@ -337,49 +331,50 @@
     span_c = {-1: (left, left + width, SIDE), 0: (left, left, width), 1: (left + width - SIDE, 0, SIDE)}
 
     def x_routes():
-        i = 0
-        routes = {-1: [], 0: [], 1: []}
-        for dl, side in [(-1, -1), (-1, 1), (1, -1), (1, 1)]:
+        routes = {-1: [], 1: []}
+        for i, dl in enumerate((-1, 1)):
             sr, dr, nr = span_r[dl]
-            sc, dc, nc = span_c[side]
-            routes[dl].append(remote(X, at(dl, side), sr, dr, nr, sc, dc, nc, i))
-            i += 1
-        return routes
-
-    def g_routes():
-        i = 4
-        routes = {-1: [], 0: [], 1: []}
-        out_src = left + ch * (width - SIDE)
-        out_dst = other * (left + width)
-        for dl in (0, -1, 1):
-            sr, dr, nr = span_r[dl]
-            if dl:
-                routes[dl].append(remote(G, at(dl, 0), sr, dr, nr, other * SIDE, other * SIDE, reach, i))
-                i += 1
-            routes[dl].append(remote(G, outward(dl), sr, dr, nr, out_src, out_dst, SIDE, i))
-            i += 1
-        return routes
-
-    def halo_start(routes, order):
+            for side in (-1, 1):
+                sc, dc, nc = span_c[side]
+                routes[dl].append(remote(X, at(dl, side), sr, dr, nr, sc, dc, nc, i))
+        return routes, {-1: (X, HALO, 2 * SIDE, 0), 1: (X, HALO, 2 * SIDE, 1)}
+
+    out_src = left + ch * (width - SIDE)
+    out_dst = other * (left + width)
+
+    def g_side():
+        copy = remote(G, outward(0), top, top, rows, out_src, out_dst, SIDE, 4)
+        return {0: [copy]}, {0: (G, rows, SIDE, 4)}
+
+    def g_rows(depth):
+        routes, whole = {}, {}
+        for n, dl in enumerate((-1, 1)):
+            i = 2 + n if depth == 0 else 5 + n
+            sr = top + depth if dl < 0 else top + rows - 1 - depth
+            dr = rows + top + depth if dl < 0 else HALO - 1 - depth
+            routes[dl] = [
+                remote(G, at(dl, 0), sr, dr, 1, other * SIDE, other * SIDE, reach, i),
+                remote(G, outward(dl), sr, dr, 1, out_src, out_dst, SIDE, i),
+            ]
+            whole[dl] = (G, 1, pitch, i)
+        return routes, whole
+
+    def halo_start(halo, order):
         for dl in order:
             def go(dl=dl):
-                for copy in routes[dl]:
+                for copy in halo[0][dl]:
                     copy.start()
 
             guarded(dl, go)
 
-    def halo_finish(routes, order):
+    def halo_finish(halo, order):
         for dl in order:
-            def sent(dl=dl):
-                for copy in routes[dl]:
-                    copy.wait_send()
-
-            def got(dl=dl):
-                for copy in routes[dl]:
-                    copy.wait_recv()
-
-            guarded(dl, sent)
-            guarded(-dl, got)
+            def whole(dl=dl):
+                buf, nr, nc, i = halo[1][dl]
+                return remote(buf, sibling, 0, 0, nr, 0, 0, nc, i)
+
+            guarded(dl, lambda: whole().wait_send())
+            guarded(-dl, lambda: whole().wait_recv())
 
     def clear_poles(buf):
         @pl.when(lat == 0)
@@ -471,13 +466,9 @@
                 row = row * f
             put_row(H3, r, row.astype(BF16).astype(F32))
 
-    pltpu.make_async_remote_copy(
-        src_ref=edge.at[0:3], dst_ref=edge.at[0:3], send_sem=edge_ss, recv_sem=edge_rs.at[0],
-        device_id=sibling, device_id_type=MESH,
-    ).wait_send()
-    edge_got(other, other).wait_recv()
-    for c in (0, 1):
-        edge_got(ch, c).wait_recv()
+    edge_got(0, 3).wait_send()
+    edge_got(1, 1).wait_recv()
+    edge_got(0, 2).wait_recv()
     for side in (0, 1):
         turned = jnp.concatenate([edge_r[side, 0], edge_r[side, 1]], axis=0).astype(F32).T.astype(BF16)
         for r in range(rows):
@@ -486,8 +477,6 @@
         put_row(X3, r, X[r].astype(F32))
     for r0 in range(HALO, rows, 2):
         hidden_rows([r0], 2)
-    swaps = []
-
     def denoise_rows(first, count):
         acc = conv(H3, 1, first, count)
         for i, r in enumerate(f + n for f in first for n in range(count)):
@@ -499,8 +488,7 @@
             DF[pl.ds(pl.multiple_of(r * cols + ch * width, width), width), :] = wide
         for f in first:
             part = pl.ds(f, count)
-            swaps.append((f, count, pair_copy(den_s.at[part], den_r.at[part], 1 + len(swaps))))
-            swaps[-1][2].start()
+            pair_copy(den_s.at[part], den_r.at[part], 1).start()
 
     inner = [([r0], min(WIDE, rows - HALO - r0)) for r0 in range(HALO, rows - HALO, WIDE)]
     outer = [([0, rows - HALO], HALO)]
@@ -512,11 +500,9 @@
         def _(dl=dl):
             pltpu.make_async_remote_copy(
                 src_ref=x_send.at[pl.ds(0, 2 * HALO)], dst_ref=x_send.at[pl.ds(0, 2 * HALO)],
-                send_sem=raw_s.at[1 if dl < 0 else 0], recv_sem=raw_r.at[0],
+                send_sem=raw_s.at[1 if dl < 0 else 0], recv_sem=raw_r.at[0 if dl < 0 else 1],
                 device_id=sibling, device_id_type=MESH,
-            ).wait_send()
-            for c in (0, 1):
-                raw_got(dl, c).wait_recv()
+            ).wait()
             for i in range(HALO):
                 side = 0 if dl < 0 else 1
                 X[side * (top + rows) + i, left : left + width] = (
@@ -530,7 +516,10 @@
         denoise_rows(first, count)
 
     own_at.wait()
-    each(n_lat - 1, lambda j: small(peer_of(j), peer_of(j), 0).wait_recv())
+    pltpu.make_async_remote_copy(
+        src_ref=pay_at.at[pl.ds(0, n_lat - 1)], dst_ref=at_s.at[pl.ds(0, n_lat - 1)], send_sem=at_ss, recv_sem=at_rs,
+        device_id=sibling, device_id_type=MESH,
+    ).wait_recv()
 
     def take_pay(j):
         peer = peer_of(j)
@@ -551,10 +540,9 @@
     split = batches == 2
     if split:
         pl.when(jnp.logical_not(middle))(lambda: take_pay(0))
-    for r0, count, swap in swaps:
-        swap.wait()
-        for r in range(r0, r0 + count):
-            DF[pl.ds(pl.multiple_of(r * cols + other * width, width), width), :] = den_r[r].astype(F32)
+    pair_copy(den_s, den_r, 1).wait()
+    for r in range(rows):
+        DF[pl.ds(pl.multiple_of(r * cols + other * width, width), width), :] = den_r[r].astype(F32)
 
     def gather(t):
         lane = lax.broadcasted_iota(I32, (half, chans), 1)
@@ -575,7 +563,7 @@
     def patch_copy(peer, landing):
         return pltpu.make_async_remote_copy(
             src_ref=pat_s.at[peer], dst_ref=pat_r.at[landing],
-            send_sem=pat_ss, recv_sem=pat_rs.at[landing],
+            send_sem=pat_ss, recv_sem=pat_rs,
             device_id={"lat": peer}, device_id_type=MESH,
         )
 
@@ -614,7 +602,8 @@
         drain(pay_at.at[others], at_s.at[others], at_ss)
         drain(pat_s.at[others], pat_r.at[others], pat_ss)
 
-    g_halo = g_routes()
+    g_halo = [g_rows(depth) for depth in range(HALO)]
+    g_edge = g_side()
 
     def observe(g, first, last):
         owners = [source_of(g * sources + i) for i in range(sources)]
@@ -633,7 +622,7 @@
             pulled = jnp.dot(normal, patches[t, k], preferred_element_type=F32) - pull.astype(F32).T
             for a in range(PH):
                 Z[pl.ds((i * PH + a) * strip + reach, PW), :] = pulled[a * PW : (a + 1) * PW]
-        for n, r in enumerate((0, 1, rows - 2, rows - 1, *range(2, rows - 2))):
+        for n, r in enumerate((0, rows - 1, 1, rows - 2, *range(2, rows - 2))):
             total = None
             for i in range(GROUP):
                 t, k = owners[i // CAP], i % CAP
@@ -649,10 +638,10 @@
             GW[span_w, :] = total
             if last:
                 G[top + r, pl.ds(pl.multiple_of(other * SIDE, SIDE), reach)] = total.astype(BF16)
-                if n == 3:
-                    halo_start(g_halo, (-1, 1))
+                if n in (1, 3):
+                    halo_start(g_halo[n // 2], (-1, 1))
         if last:
-            halo_start(g_halo, (0,))
+            halo_start(g_edge, (0,))
 
     if split:
         pl.when(middle)(lambda: take_from(0))
@@ -678,28 +667,34 @@
                 row = row * f
             put_row(H3, r, row.astype(BF16).astype(F32))
 
-    halo_finish(g_halo, (0,))
+    halo_finish(g_edge, (0,))
     for r in range(top, top + rows):
         put_row(X3, r, G[r].astype(F32))
     for r0 in range(HALO, rows, 2):
         grad_rows([r0], 2)
-    back_home = []
-
-    def finish_rows(first, count):
+
+    def finish_rows(first, count, sem):
         acc = conv(H3, 3, first, count)
-        for i, r in enumerate(f + n for f in first for n in range(count)):
+        order = [f + n for f in first for n in range(count)]
+        kept = []
+        for i, r in enumerate(order):
             grad = GW[r * pitch + left : r * pitch + left + width, :] + acc[i * pitch + left : i * pitch + left + width]
             res = (base[r * width : (r + 1) * width, :] - guide_rate * grad).T
             out_s[r] = jnp.where(ch == 0, res[half:chans], res[0:half]).astype(BF16)
-            out_h[0, pl.ds(r, half, stride=rows), :] = jnp.where(ch == 0, res[0:half], res[half:chans])
+            kept.append(jnp.where(ch == 0, res[0:half], res[half:chans]))
         for f in first:
             part = pl.ds(f, count)
-            back_home.append((f, count, pair_copy(out_s.at[part], out_r.at[part], 1 + len(swaps) + len(back_home))))
-            back_home[-1][2].start()
+            pair_copy(out_s.at[part], out_r.at[part], sem).start()
+        for r, mine_r in zip(order, kept):
+            out_h[0, pl.ds(r, half, stride=rows), :] = mine_r
 
     for first, count in inner:
-        finish_rows(first, count)
-    each(n_lat - 1, lambda j: patch_copy(peer_of(j), peer_of(j)).wait_recv())
+        finish_rows(first, count, 2)
+    others = pl.ds(0, n_lat - 1)
+    pltpu.make_async_remote_copy(
+        src_ref=pat_s.at[others], dst_ref=pat_r.at[others], send_sem=pat_ss, recv_sem=pat_rs,
+        device_id=sibling, device_id_type=MESH,
+    ).wait_recv()
     drain_all()
 
     def innovate(b):
@@ -710,19 +705,22 @@
         inn_out[b] = (predicted[0:half] - values[b].astype(F32)).astype(BF16)
 
     each(blocks, innovate)
-    halo_finish(g_halo, (-1, 1))
-    for r in (0, 1, top + rows, top + rows + 1):
-        put_row(X3, r, G[r].astype(F32))
-    grad_rows([0, rows], HALO)
-    for first, count in outer:
-        finish_rows(first, count)
+    for depth in range(HALO):
+        halo_finish(g_halo[depth], (-1, 1))
+        for r in (HALO - 1 - depth, top + rows + depth):
+            put_row(X3, r, G[r].astype(F32))
+        grad_rows([HALO - 1 - depth, rows + depth], 1)
+        finish_rows([HALO - 1 - depth, rows - HALO + depth], 1, 3)
     mine = pl.ds(pl.multiple_of(ch * width, width), width)
     theirs = pl.ds(pl.multiple_of(other * width, width), width)
     out[:, mine] = out_h[0]
 
-    for r0, count, copy in back_home:
-        copy.wait()
-        for r in range(r0, r0 + count):
+    middle_rows = tuple(range(HALO, rows - HALO))
+    edge_rows = (*range(HALO), *range(rows - HALO, rows))
+    for sem, which in ((2, middle_rows), (3, edge_rows)):
+        part = pl.ds(0, len(which))
+        pair_copy(out_s.at[part], out_r.at[part], sem).wait()
+        for r in which:
             out_h[1, pl.ds(r, half, stride=rows), :] = out_r[r].astype(F32)
     out[:, theirs] = out_h[1]
 
@@ -748,7 +746,6 @@
     pitch = width + 2 * SIDE
     reach = width + SIDE
     px = rows * width
-    pairs = 1 + 2 * (2 - (HALO + HALO - rows) // WIDE)
     vmem = pl.BlockSpec(memory_space=pltpu.VMEM)
     hbm = pl.BlockSpec(memory_space=pltpu.HBM)
     dma = pltpu.SemaphoreType.DMA
@@ -780,8 +777,8 @@
             pltpu.VMEM((4, half, width), BF16),
             pltpu.VMEM((2, 2, half, width), BF16),
             pltpu.VMEM((2, 2, HALO, half, width), BF16),
-            dma, dma((4,)),
-            dma((2,)), dma((4,)),
+            dma, dma((2,)),
+            dma((2,)), dma((2,)),
             pltpu.VMEM((rows + 4, pitch, chans), BF16),
             pltpu.VMEM(((rows + 4) * pitch, 3 * chans), BF16),
             pltpu.VMEM(((rows + 2) * pitch, 3 * chans), BF16),
@@ -811,15 +808,15 @@
             pltpu.SMEM((blocks,), I32),
             pltpu.SemaphoreType.REGULAR,
             pltpu.SemaphoreType.REGULAR,
-            dma((9,)), dma((9,)),
-            dma((pairs,)), dma((pairs,)),
+            dma((7,)), dma((7,)),
+            dma((4,)), dma((4,)),
             dma, dma((n_lat,)),
-            dma, dma((n_lat,)),
+            dma, dma,
             dma, dma((n_lat,)),
             dma, dma((n_lat,)),
             dma,
             dma,
-            dma, dma((n_lat,)),
+            dma, dma,
         ],
         compiler_params=pltpu.CompilerParams(
             collective_id=0, has_side_effects=True, vmem_limit_bytes=(63 if slots <= 2 * GROUP else 48) * 1024 * 1024

time: 23.4 us -> 22.9 us (0.979)
  Pallas kernels: 22.6 us -> 22.1 us
    pallas_call x1, Pallas kernels: 21.8 us -> 21.3 us  [body(): call(dest_tile, row_offset, col_offset, noisy_state, kernel_in, kernel_ou...]
where the time goes in v6:
time: 22.9 us; the launch traced here: 22.8 us
  Pallas kernels  22.1 us (97%)
  between operations  0.64 us (3%)
    pallas_call x1, Pallas kernels, body(): call(dest_tile, row_offset, col_offset, noisy_state, kernel_in, kernel_ou...  21.3 us
    pallas_call x1, Pallas kernels, body(): pl.pallas_call(store, out_shape=(jax.ShapeDtypeStruct((half * rows, cols)...  0.82 us

profile of v6, /device:TPU:0, one launch (start us, length us, event | category | flops | bytes accessed | tf_op | source)
XLA Modules:
  0.0 22.8 jit_solution(8659904150265455615)
XLA Ops:
  0.6 21.3 %shard_map.113 = (f32[512,256]{1,0:T(8,128)S(1)}, bf16[4,64,128]{2,1,0:T(8,128)(2,1)S(1)}) custom-call(s32[4]{0:T(128)} %dest_hbm.1, s32[4]{0:T(128)} %row_hbm.1, s32[4]{0:T(128)} %col_hbm.1, bf16[64,8,256]{2,1,0:T(8,128)(2,1)} %x_hbm.1, bf16[3,3,128,128]{3,2,1,0:T(8,128)(2,1)} %kin_hbm.1, bf16[3,3,128,128]{3,2,1,0:T(8,128)(2,1)} %kout_hbm.1, ...), custom_call_target="tpu_custom_call" | custom-call | tf_op jit(solution)/shard_map/pallas_call | solution.py:825
  21.9 0.8 %shard_map.114 = (f32[512,256]{1,0:T(8,128)}, bf16[4,64,128]{2,1,0:T(8,128)(2,1)}) custom-call(f32[512,256]{1,0:T(8,128)S(1)} %get-tuple-element.6.out, bf16[4,64,128]{2,1,0:T(8,128)(2,1)S(1)} %get-tuple-element.7.innovation), custom_call_target="tpu_custom_call" | custom-call | tf_op jit(solution)/shard_map/pallas_call | solution.py:829

commit v7 on v6

--- a/solution.py
+++ b/solution.py
@@ -690,21 +690,6 @@
 
     for first, count in inner:
         finish_rows(first, count, 2)
-    others = pl.ds(0, n_lat - 1)
-    pltpu.make_async_remote_copy(
-        src_ref=pat_s.at[others], dst_ref=pat_r.at[others], send_sem=pat_ss, recv_sem=pat_rs,
-        device_id=sibling, device_id_type=MESH,
-    ).wait_recv()
-    drain_all()
-
-    def innovate(b):
-        slot = plan[b]
-        part = pat_r[slot // CAP, slot % CAP].astype(F32)
-        patch = jnp.concatenate([part, pltpu.roll(part, half, 1)], axis=0).astype(BF16)
-        predicted = jnp.dot(weight[b], patch, preferred_element_type=F32).T
-        inn_out[b] = (predicted[0:half] - values[b].astype(F32)).astype(BF16)
-
-    each(blocks, innovate)
     for depth in range(HALO):
         halo_finish(g_halo[depth], (-1, 1))
         for r in (HALO - 1 - depth, top + rows + depth):
@@ -715,6 +700,21 @@
     theirs = pl.ds(pl.multiple_of(other * width, width), width)
     out[:, mine] = out_h[0]
 
+    others = pl.ds(0, n_lat - 1)
+    pltpu.make_async_remote_copy(
+        src_ref=pat_s.at[others], dst_ref=pat_r.at[others], send_sem=pat_ss, recv_sem=pat_rs,
+        device_id=sibling, device_id_type=MESH,
+    ).wait_recv()
+    drain_all()
+
+    def innovate(b):
+        slot = plan[b]
+        part = pat_r[slot // CAP, slot % CAP].astype(F32)
+        patch = jnp.concatenate([part, pltpu.roll(part, half, 1)], axis=0).astype(BF16)
+        predicted = jnp.dot(weight[b], patch, preferred_element_type=F32).T
+        inn_out[b] = (predicted[0:half] - values[b].astype(F32)).astype(BF16)
+
+    each(blocks, innovate)
     middle_rows = tuple(range(HALO, rows - HALO))
     edge_rows = (*range(HALO), *range(rows - HALO, rows))
     for sem, which in ((2, middle_rows), (3, edge_rows)):

time: 22.9 us -> 22.8 us (level)
  no operation moved by 1% of the time
where the time goes in v7:
time: 22.8 us; the launch traced here: 22.6 us
  Pallas kernels  22 us (96%)
  between operations  0.64 us (3%)
    pallas_call x1, Pallas kernels, body(): call(dest_tile, row_offset, col_offset, noisy_state, kernel_in, kernel_ou...  21.2 us
    pallas_call x1, Pallas kernels, body(): pl.pallas_call(store, out_shape=(jax.ShapeDtypeStruct((half * rows, cols)...  0.82 us

profile of v7, /device:TPU:0, one launch (start us, length us, event | category | flops | bytes accessed | tf_op | source)
XLA Modules:
  0.0 22.6 jit_solution(521880934699215241)
XLA Ops:
  0.6 21.2 %shard_map.113 = (f32[512,256]{1,0:T(8,128)S(1)}, bf16[4,64,128]{2,1,0:T(8,128)(2,1)S(1)}) custom-call(s32[4]{0:T(128)} %dest_hbm.1, s32[4]{0:T(128)} %row_hbm.1, s32[4]{0:T(128)} %col_hbm.1, bf16[64,8,256]{2,1,0:T(8,128)(2,1)} %x_hbm.1, bf16[3,3,128,128]{3,2,1,0:T(8,128)(2,1)} %kin_hbm.1, bf16[3,3,128,128]{3,2,1,0:T(8,128)(2,1)} %kout_hbm.1, ...), custom_call_target="tpu_custom_call" | custom-call | tf_op jit(solution)/shard_map/pallas_call | solution.py:825
  21.8 0.8 %shard_map.114 = (f32[512,256]{1,0:T(8,128)}, bf16[4,64,128]{2,1,0:T(8,128)(2,1)}) custom-call(f32[512,256]{1,0:T(8,128)S(1)} %get-tuple-element.6.out, bf16[4,64,128]{2,1,0:T(8,128)(2,1)S(1)} %get-tuple-element.7.innovation), custom_call_target="tpu_custom_call" | custom-call | tf_op jit(solution)/shard_map/pallas_call | solution.py:829
